TPU v7x, 8 devices: a whole 2x2x1 slice. The times are simulated.
8 devices in a mesh: dp: 1 (over z), tp: 2 (over y), cp: 4 (over x, core).
Axes of the slice: x: 2, y: 2, z: 1, core: 2. Of those that a mesh axis runs over, the one named last changes fastest.
Arguments:
- hidden: bfloat16 [24, 768, 512], P('dp', 'cp')
- tokens: int32 [24, 768], P('dp', 'cp')
- emb_table: bfloat16 [50304, 512], P('tp')
- out_table: bfloat16 [50304, 512], P('tp')
- w_proj: bfloat16 [512, 1024], replicated
- gain_h: float32 [512], replicated
- gain_e: float32 [512], replicated
- gain_f: float32 [512], replicated
Outputs:
- output 1: float32 [1], P('dp')
- output 2: bfloat16 [24, 768, 512], P('dp', 'cp')
- output 3: float32 [512, 1024], P('dp')
- output 4: float32 [50304, 512], P(('dp', 'tp'))
- output 5: float32 [50304, 512], P(('dp', 'tp'))
- output 6: float32 [512], P('dp')
- output 7: float32 [512], P('dp')
- output 8: float32 [512], P('dp')
All inputs are finite; a program needn't handle non-finite values.
Results may differ from a plain program's by a relative error of at most 0.001.
Values sent between devices are 32-bit elements.
A program may use at most 1 GiB of HBM per device.

v0:
```python
import jax
import jax.numpy as jnp
from jax import lax
from jax.sharding import PartitionSpec as P

MTP_WEIGHT = 0.3
NORM_EPS = 1e-6


def rms_norm(values, gain):
    scale = lax.rsqrt(jnp.mean(values * values, axis=-1, keepdims=True) + NORM_EPS)
    return values * scale * gain


def solution(mesh):
    cp_size = mesh.shape["cp"]
    shift_pairs = [(src + 1, src) for src in range(cp_size - 1)]

    def local_step(hidden, tokens, emb_blk, out_blk, w_proj, gain_h, gain_e, gain_f):
        batch, piece_len, width = hidden.shape
        vocab_blk = emb_blk.shape[0]
        tp_rank = lax.axis_index("tp")
        cp_rank = lax.axis_index("cp")
        seq_len = piece_len * cp_size
        next_head = lax.ppermute(tokens[:, :2], "cp", shift_pairs)
        ext_ids = jnp.concatenate([tokens, next_head], axis=1)
        next_ids = ext_ids[:, 1:piece_len + 1]
        label_ids = ext_ids[:, 2:]
        positions = cp_rank * piece_len + jnp.arange(piece_len)
        pos_weight = (positions < seq_len - 2).astype(jnp.float32)
        local_next = next_ids - tp_rank * vocab_blk
        in_block = (local_next >= 0) & (local_next < vocab_blk)
        emb_rows = jnp.take(emb_blk, jnp.clip(local_next, 0, vocab_blk - 1), axis=0).astype(jnp.float32)
        emb_rows = jnp.where(in_block[..., None], emb_rows, 0.0)
        emb_full = lax.psum(emb_rows, "tp")
        norm_h, vjp_h = jax.vjp(rms_norm, hidden.astype(jnp.float32), gain_h)
        norm_e, vjp_e = jax.vjp(rms_norm, emb_full, gain_e)
        joined = jnp.concatenate([norm_h.astype(jnp.bfloat16), norm_e.astype(jnp.bfloat16)], axis=-1)
        mixed = jnp.einsum("bsk,nk->bsn", joined, w_proj, preferred_element_type=jnp.float32)
        normed, vjp_f = jax.vjp(rms_norm, mixed, gain_f)
        features = normed.astype(jnp.bfloat16)
        logits = jnp.einsum("bsd,vd->bsv", features, out_blk, preferred_element_type=jnp.float32)
        row_max = lax.pmax(jnp.max(logits, axis=-1), "tp")
        local_label = label_ids - tp_rank * vocab_blk
        is_label = jnp.arange(vocab_blk) == local_label[..., None]
        exp_part = jnp.sum(jnp.exp(logits - row_max[..., None]), axis=-1)
        label_part = jnp.sum(jnp.where(is_label, logits, 0.0), axis=-1)
        exp_sum, label_logit = lax.psum((exp_part, label_part), "tp")
        log_norm = row_max + jnp.log(exp_sum)
        loss_part = jnp.sum(pos_weight * (log_norm - label_logit))
        soft_prob = jnp.exp(logits - log_norm[..., None])
        grad_logits = (MTP_WEIGHT * pos_weight[:, None] * (soft_prob - is_label.astype(jnp.float32))).astype(jnp.bfloat16)
        d_out = jnp.einsum("bsv,bsd->vd", grad_logits, features, preferred_element_type=jnp.float32)
        d_feats = lax.psum(jnp.einsum("bsv,vd->bsd", grad_logits, out_blk, preferred_element_type=jnp.float32), "tp")
        d_mixed, d_gain_f = vjp_f(d_feats)
        d_mixed_b = d_mixed.astype(jnp.bfloat16)
        d_proj = jnp.einsum("bsn,bsk->nk", d_mixed_b, joined, preferred_element_type=jnp.float32)
        d_joined = jnp.einsum("bsn,nk->bsk", d_mixed_b, w_proj, preferred_element_type=jnp.float32)
        d_hid, d_gain_h = vjp_h(d_joined[..., :width])
        d_embrow, d_gain_e = vjp_e(d_joined[..., width:])
        seg_ids = jnp.where(in_block, local_next, vocab_blk).reshape(-1)
        d_emb = jax.ops.segment_sum(d_embrow.reshape(-1, width), seg_ids, num_segments=vocab_blk)
        cp_totals = lax.psum((d_out, d_emb, d_proj, d_gain_h, d_gain_e, d_gain_f, loss_part), "cp")
        d_out, d_emb, d_proj, d_gain_h, d_gain_e, d_gain_f, loss_sum = cp_totals
        loss = (MTP_WEIGHT * loss_sum / (batch * (seq_len - 2))).reshape(1)
        return loss, d_hid.astype(jnp.bfloat16), d_proj, d_emb, d_out, d_gain_h, d_gain_e, d_gain_f

    part_seq = P("dp", "cp", None)
    in_specs = (part_seq, P("dp", "cp"), P("tp", None), P("tp", None), P(None, None), P(None), P(None), P(None))
    out_specs = (P("dp"), part_seq, P("dp", None), P(("dp", "tp"), None), P(("dp", "tp"), None), P("dp"), P("dp"), P("dp"))
    return jax.shard_map(local_step, mesh=mesh, in_specs=in_specs, out_specs=out_specs, check_vma=False)
```

profile of v0, /device:TPU:1, one launch (start us, length us, event | category | flops | bytes accessed | tf_op | source)
XLA Modules:
  0.0 3078.9 jit_solution(289384223184867834)
XLA Ops:
  7.2 0.0 copy-start
  7.2 0.0 all-reduce.7.cloned.1.call-start
  7.2 0.8 slice.15
  8.0 1.9 collective-permute-start
  9.9 3.9 collective-permute-done
  13.9 1.5 broadcast_select_fusion
  15.4 0.1 reshape.109
  15.5 25.8 gather_fusion
  41.4 7.4 convert_select_fusion
  48.8 0.0 all-reduce.7.cloned.1.call-update
  48.8 0.2 all-reduce.9.cloned.1.call-start
  49.1 0.6 fusion.24
  49.6 0.6 fusion.25
  50.2 3.4 fusion.12
  53.6 0.0 copy-start.14
  53.6 0.6 copy-done.11
  54.2 4.5 fusion.8
  58.7 0.7 reshape.117
  59.4 203.6 %all-reduce.7.cloned.1.call-done = f32[24,192,512]{2,1,0:T(8,128)} async-done(((f32[24,192,512]{2,1,0:T(8,128)}), f32[24,192,512]{2,1,0:T(8,128)}) %all-reduce.7.cloned.1.call-update) | async-done | bytes 9437200 | tf_op jit(solution)/shard_map/psum | solution.py:35
  263.1 4.7 multiply_reduce_fusion.5
  267.8 0.0 slice-start.5
  267.8 0.6 copy-done.16
  268.4 0.6 copy-done.9
  269.0 0.4 copy-done.1
  269.4 1.0 multiply_convert_fusion.2
  270.5 0.2 slice-done.5
  270.7 0.3 slice-done.6
  271.0 5.2 multiply_reduce_fusion.4
  276.3 0.0 copy-start.2
  276.3 3.7 copy-done.2
  280.0 2.7 multiply_convert_fusion.4.clone.4
  282.7 158.8 %fusion.28 = (f32[24,192]{1,0:T(8,128)S(1)}, f32[24,192,25152]{2,1,0:T(8,128)}) fusion(bf16[25152,512]{1,0:T(8,128)(2,1)} %param.11, bf16[24,192,512]{2,1,0:T(8,128)(2,1)} %multiply_convert_fusion.4.clone.4), kind=kOutput, calls=%fused_computation.70 | convolution fusion | flops 118797918208 | bytes 494094336 | tf_op jit(solution)/shard_map/bsd,vd->bsv/dot_general | solution.py:42
  441.6 5.7 pmax.7
  447.3 0.0 copy-start.26
  447.3 0.0 copy-start.27
  447.3 155.5 %select_reduce_fusion = (f32[24,192]{1,0:T(8,128)S(1)}, f32[24,192]{1,0:T(8,128)S(1)}) fusion(f32[24,192,25152]{2,1,0:T(8,128)} %get-tuple-element.39, s32[24,192]{1,0:T(8,128)S(1)} %copy-done.13, f32[24,192]{1,0:T(8,128)S(1)} %pmax.7), kind=kLoop, calls=%fused_computation.3 | loop fusion | flops 579492864 | bytes 463675392 | tf_op jit(solution)/shard_map/reduce_sum | solution.py:47
  602.9 6.2 all-reduce.2
  609.0 0.6 multiply_reduce_fusion.6
  609.6 218.9 %multiply_convert_fusion = bf16[24,192,25152]{2,1,0:T(8,128)(2,1)} fusion(f32[24,192,25152]{2,1,0:T(8,128)} %get-tuple-element.39, f32[24,192]{1,0:T(8,128)S(1)} %get-tuple-element.30, f32[192]{0:T(256)S(1)} %copy-done.27, s32[24,192]{1,0:T(8,128)S(1)} %copy-done.13), kind=kLoop, calls=%fused_computation.2 | loop fusion | flops 695402496 | bytes 695440128 | tf_op jit(solution)/shard_map/convert_element_type | solution.py:52
  828.5 135.3 %fusion = f32[24,192,512]{2,1,0:T(8,128)} fusion(bf16[24,192,25152]{2,1,0:T(8,128)(2,1)} %multiply_convert_fusion, bf16[25152,512]{1,0:T(8,128)(2,1)} %param.11), kind=kOutput, calls=%fused_computation.7 | convolution fusion | flops 118682025984 | bytes 266993664 | tf_op jit(solution)/shard_map/bsv,vd->bsd/dot_general | solution.py:54
  963.8 0.0 all-reduce.9.cloned.1.call-update
  963.9 0.0 all-reduce.11.cloned.1.call-start
  963.9 0.7 copy-done.8
  964.6 135.7 %convolution_bitcast_fusion = f32[25152,512]{1,0:T(8,128)} fusion(bf16[24,192,25152]{2,1,0:T(8,128)(2,1)} %multiply_convert_fusion, f32[24,192,512]{2,1,0:T(8,128)} %copy-done.2, f32[512]{0:T(512)S(1)} %copy-done.25, f32[24,192]{1,0:T(8,128)S(1)} %copy-done.8), kind=kOutput, calls=%fused_computation.6 | convolution fusion | flops 118689103872 | bytes 292769792 | tf_op jit(solution)/shard_map/bsv,bsd->vd/dot_general | solution.py:53
  1100.3 82.7 %all-reduce.9.cloned.1.call-done = f32[24,192,512]{2,1,0:T(8,128)} async-done(((f32[24,192,512]{2,1,0:T(8,128)}), f32[24,192,512]{2,1,0:T(8,128)}) %all-reduce.9.cloned.1.call-update) | async-done | bytes 9437200 | tf_op jit(solution)/shard_map/psum | solution.py:54
  1182.9 9.4 multiply_reduce_fusion
  1192.4 2.4 copy-done.4
  1194.8 3.7 fusion.10
  1198.5 0.0 slice-start
  1198.5 0.0 slice-start.1
  1198.5 0.0 slice-start.4
  1198.5 9.9 fusion.16
  1208.5 0.0 copy-start.21
  1208.5 0.0 copy-start.23
  1208.5 9.8 fusion.17
  1218.5 9.3 multiply_reduce_fusion.1
  1227.9 13.8 add_add_fusion
  1241.7 49.0 %scatter_custom_fusion = f32[25152,512]{1,0:T(8,128)} fusion(s32[4608]{0:T(1024)} %reshape.117, f32[4608,512]{1,0:T(8,128)} %bitcast.34, f32[]{:T(128)} %constant.21.clone.1), kind=kCustom, calls=%fused_computation.11 | custom fusion | flops 2359296 | bytes 51511808 | tf_op jit(solution)/shard_map/scatter-add | solution.py:62
  1290.7 0.0 all-reduce.11.cloned.1.call-update
  1290.7 6.7 all-reduce
  1298.1 1699.7 %all-reduce.11.cloned.1.call-done = (f32[512,1024]{1,0:T(8,128)}, f32[25152,512]{1,0:T(8,128)}, f32[25152,512]{1,0:T(8,128)}) async-done(((f32[512,1024]{1,0:T(8,128)}, f32[25152,512]{1,0:T(8,128)}, f32[25152,512]{1,0:T(8,128)}), (f32[512,1024]{1,0:T(8,128)}, f32[25152,512]{1,0:T(8,128)}, f32[25152,512]{1,0:T(8,128)})) %all-reduce.11.cloned.1.call-update) | async-done | bytes 105119760 | tf_op jit(solution)/shard_map/psum | solution.py:63
  2997.8 3.2 copy.21
  3001.0 35.0 %copy.22 = f32[25152,512]{1,0:T(8,128)} copy(f32[25152,512]{1,0:T(8,128)} %get-tuple-element.45) | data formatting | bytes 103022592
  3036.0 35.0 %copy.23 = f32[25152,512]{1,0:T(8,128)} copy(f32[25152,512]{1,0:T(8,128)} %get-tuple-element.46) | data formatting | bytes 103022592
  (66 shorter events, 0.2 us)
Async XLA Ops:
  7.2 263.3 %copy-start = (bf16[512,1024]{1,0:T(8,128)(2,1)S(1)}, bf16[512,1024]{1,0:T(8,128)(2,1)}, u32[]{:S(2)}) copy-start(bf16[512,1024]{1,0:T(8,128)(2,1)} %param.12) | copy-start | bytes 3145732
  7.2 255.9 %all-reduce.7.cloned.1.call-start = ((), (), s32[]{:S(2)}) async-start(), calls=%async_computation | async-start | bytes 18874368 | tf_op jit(solution)/shard_map/psum | solution.py:35
  8.0 5.9 collective-permute-start
  48.8 5.4 copy-start.22
  48.8 1134.1 %all-reduce.9.cloned.1.call-start = ((), (), s32[]{:S(2)}) async-start(), calls=%async_computation.1 | async-start | bytes 18874368 | tf_op jit(solution)/shard_map/psum | solution.py:54
  53.6 5.1 copy-start.14
  53.6 0.6 copy-start.11
  54.2 214.7 %copy-start.20 = (f32[512]{0:T(512)S(1)}, f32[512]{0:T(512)}, u32[]{:S(2)}) copy-start(f32[512]{0:T(512)} %param.14) | copy-start | bytes 6148
  263.0 6.4 copy-start.1
  267.8 0.6 copy-start.16
  267.8 2.9 slice-start.5
  268.4 0.6 copy-start.9
  269.4 1.6 slice-start.6
  271.0 5.2 copy-start.5
  271.0 9.0 copy-start.24
  276.3 3.7 copy-start.2
  276.3 3.7 copy-start.18
  276.3 3.7 copy-start.7
  282.7 164.6 %copy-start.13 = (s32[24,192]{1,0:T(8,128)S(1)}, s32[24,192]{1,0:T(8,128)}, u32[]{:S(2)}) copy-start(s32[24,192]{1,0:T(8,128)} %get-tuple-element.33) | copy-start | bytes 55300
  447.3 161.7 %copy-start.26 = (f32[192]{0:T(256)S(1)}, f32[192]{0:T(256)}, u32[]{:S(2)}) copy-start(f32[192]{0:T(256)} %fusion.25) | copy-start | bytes 2308
  447.3 162.3 %copy-start.27 = (f32[192]{0:T(256)S(1)}, f32[192]{0:T(256)}, u32[]{:S(2)}) copy-start(f32[192]{0:T(256)} %fusion.24) | copy-start | bytes 2308
  963.8 0.7 copy-start.8
  963.8 0.7 copy-start.25
  963.9 2034.0 %all-reduce.11.cloned.1.call-start = ((), (), s32[]{:S(2)}) async-start(), calls=%async_computation.2 | async-start | bytes 210239488 | tf_op jit(solution)/shard_map/psum | solution.py:63
  1100.3 92.1 %copy-start.19 = (f32[24,192]{1,0:T(8,128)S(1)}, f32[24,192]{1,0:T(8,128)}, u32[]{:S(2)}) copy-start(f32[24,192]{1,0:T(8,128)} %copy-done.18) | copy-start | bytes 55300
  1182.9 9.5 copy-start.3
  1182.9 11.9 copy-start.4
  1182.9 15.6 slice-start.7
  1194.8 3.7 slice-start.8
  1194.8 23.6 slice-start.3
  1198.5 10.0 copy-start.6
  1198.5 19.9 slice-start
  1198.5 19.9 slice-start.1
  1198.5 19.9 slice-start.4
  1208.5 9.9 slice-start.2
  1208.5 9.9 copy-start.10
  1208.5 9.9 copy-start.12
  1208.5 9.9 copy-start.21
  1208.5 9.9 copy-start.23
  1218.5 9.3 copy-start.15
  1218.5 9.3 copy-start.17
Sparse Core Ops, SparseCore 0:
  48.9 214.0 all-reduce.6
  964.0 218.9 all-reduce.8
  1290.8 1706.9 all-reduce.10
where the time goes:
time: 3080 us
  waiting for transfers between devices  1990 us (65%)
  other arithmetic  487 us (16%)
  matrix products  455 us (15%)
  local copies, waits for them, and re-layouts  110 us (4%)
    psum x1, waiting for transfers between devices, local_step(): lax.psum((d_out, d_emb, d_proj, d_gain_h, d_gain_e, d_gain_f, loss_part),...  1700 us
    convert_element_type x1, other arithmetic, local_step(): (MTP_WEIGHT * pos_weight[:, None] * (soft_prob - is_label.astype(jnp.floa...  219 us
    psum x1, waiting for transfers between devices, local_step(): emb_full = lax.psum(emb_rows, 'tp')  204 us
    dot_general x1, matrix products, local_step(): jnp.einsum('bsd,vd->bsv', features, out_blk, preferred_element_type=jnp.f...  159 us
    reduce_sum x1, other arithmetic, local_step(): label_part = jnp.sum(jnp.where(is_label, logits, 0.0), axis=-1)  156 us
    dot_general x1, matrix products, local_step(): jnp.einsum('bsv,bsd->vd', grad_logits, features, preferred_element_type=j...  136 us
    dot_general x1, matrix products, local_step(): jnp.einsum('bsv,vd->bsd', grad_logits, out_blk, preferred_element_type=jn...  135 us
    unnamed x77, local copies, waits for them, and re-layouts  82.8 us
  transfers between devices with their start and end apart: 4, of which 4 were waited for; matrix products, arithmetic and copies ran while one was open for 5% of the time, Pallas kernels for 0%

commit v1 on v0

v1 whole, which is shorter than its diff:
```python
import functools

import jax
import jax.numpy as jnp
from jax import lax
from jax.experimental import pallas as pl
from jax.experimental.pallas import tpu as pltpu
from jax.sharding import PartitionSpec as P


MTP_WEIGHT = 0.3
NORM_EPS = 1e-6
LOG2E = 1.4426950408889634
LN2 = 0.6931471805599453
NEG = -1e30
V_TILE = 2096
N_CHUNK = 3
N_PART = 3
VMEM_BYTES = 67043328
f32, bf16 = jnp.float32, jnp.bfloat16
NT = (((1,), (1,)), ((), ()))
NN = (((1,), (0,)), ((), ()))
TN = (((0,), (0,)), ((), ()))
CORE_SWAP = [(0, 1), (1, 0), (2, 3), (3, 2)]
X_SWAP = [(0, 2), (2, 0), (1, 3), (3, 1)]
Y_SWAP = [(0, 1), (1, 0)]


def cuts(size, pieces, step):
    edges = [((size * i) // pieces) // step * step for i in range(pieces)] + [size]
    return list(zip(edges[:-1], edges[1:]))


def tree(op, items):
    items = list(items)
    while len(items) > 1:
        items = [op(items[i], items[i + 1]) if i + 1 < len(items) else items[i] for i in range(0, len(items), 2)]
    return items[0]


def alternate(first, second):
    out = []
    for i in range(max(len(first), len(second))):
        out += first[i:i + 1] + second[i:i + 1]
    return out


def interleave(dots, passes):
    done = 0
    for i, dot in enumerate(dots):
        dot()
        while done < len(passes) and (done + 1) * len(dots) <= (i + 1) * len(passes):
            passes[done]()
            done += 1
    for piece in passes[done:]:
        piece()


def grad_piece(y_ref, g_ref, lab_ref, le_ref, wt_ref, hit_ref, base, row0, lanes, scale, l, r0, r1):
    sl = pl.ds(pl.multiple_of(base + l, lanes), lanes)
    lab = lab_ref[:, sl] - (lax.broadcasted_iota(jnp.int32, (8, lanes), 0) + row0)
    le = jnp.broadcast_to(le_ref[:, sl], (8, lanes))
    wt = jnp.broadcast_to(wt_ref[:, sl], (8, lanes))
    if hit_ref is not None:
        acc = [hit_ref[:8, sl], hit_ref[8:, sl]]
    for r in range(r0, r1, 16):
        halves = []
        for q in (0, 8):
            y = y_ref[r + q:r + q + 8, l:l + lanes]
            if scale:
                y = y * LOG2E
            hit = lab == (r + q)
            e = jnp.exp2(y - le)
            halves.append(jnp.where(hit, e - wt, e))
            if hit_ref is not None:
                acc[q // 8] = jnp.where(hit, y, acc[q // 8])
        g_ref[r:r + 16, l:l + lanes] = jnp.concatenate(halves, axis=0).astype(bf16)
    if hit_ref is not None:
        hit_ref[:8, sl] = acc[0]
        hit_ref[8:, sl] = acc[1]


def once():
    return dict(pipeline_mode=pl.Buffered(1))


def params():
    return pltpu.CompilerParams(vmem_limit_bytes=VMEM_BYTES)


def cost(dots, rows, n, extra):
    return pl.CostEstimate(flops=2 * dots * rows * n * 512, bytes_accessed=extra, transcendentals=rows * n)


def rms_parts(x):
    return lax.rsqrt(jnp.mean(x * x, axis=-1, keepdims=True) + NORM_EPS)


def rms_back(dy, x, r, gain):
    dg = dy * gain
    dx = r * dg - x * (r * r * r) * jnp.mean(dg * x, axis=-1, keepdims=True)
    n, width = x.shape
    return dx, jnp.sum((dy * x * r).reshape(n // 8, 8, width), axis=0)


def mix(h_ref, own_ref, recv_ref, w_ref, g_ref):
    h = h_ref[...].astype(f32)
    e = own_ref[...] + recv_ref[...]
    rh, re = rms_parts(h), rms_parts(e)
    joined = jnp.concatenate([(h * rh * g_ref[0:1, :]).astype(bf16), (e * re * g_ref[1:2, :]).astype(bf16)], axis=1)
    mixed = lax.dot_general(joined, w_ref[...], NT, preferred_element_type=f32)
    return h, e, rh, re, joined, mixed, rms_parts(mixed)


def tiles_of(tile, *widths):
    return [pl.BlockSpec((tile, w), lambda i: (i, 0)) for w in widths]


def front_kernel(hid, own, recv, w_proj, gains):
    n, width = hid.shape
    tile = 512

    def body(h_ref, own_ref, recv_ref, w_ref, g_ref, out_ref):
        mixed, rf = mix(h_ref, own_ref, recv_ref, w_ref, g_ref)[5:]
        out_ref[...] = mixed * rf * g_ref[2:3, :]

    return pl.pallas_call(
        body,
        grid=(n // tile,),
        in_specs=tiles_of(tile, width, width, width) + [
            pl.BlockSpec((width, 2 * width), lambda i: (0, 0)), pl.BlockSpec((3, width), lambda i: (0, 0))],
        out_specs=tiles_of(tile, width)[0],
        out_shape=jax.ShapeDtypeStruct((n, width), f32),
        compiler_params=params(),
        cost_estimate=pl.CostEstimate(flops=4 * n * width * width, bytes_accessed=14 * n * width, transcendentals=3 * n),
        name="front",
    )(hid, own, recv, w_proj, gains)


def back_kernel(hid, own, recv, w_proj, gains, df_mine, df_recv, totals):
    n, width = hid.shape
    tile = 512

    def body(h_ref, own_ref, recv_ref, w_ref, g_ref, a_ref, b_ref, *rest):
        dh_ref, de_ref, dw_ref, dg_ref = rest[-4:]
        h, e, rh, re, joined, mixed, rf = mix(h_ref, own_ref, recv_ref, w_ref, g_ref)
        df = (a_ref[...] + b_ref[...]).T
        du, dgf = rms_back(df, mixed, rf, g_ref[2:3, :])
        du = du.astype(bf16)
        dx = lax.dot_general(du, w_ref[...], NN, preferred_element_type=f32)
        dh, dgh = rms_back(dx[:, :width], h, rh, g_ref[0:1, :])
        de, dge = rms_back(dx[:, width:], e, re, g_ref[1:2, :])
        dh_ref[...] = dh.astype(bf16)
        de_ref[...] = de
        dw = lax.dot_general(du, joined, TN, preferred_element_type=f32)

        @pl.when(pl.program_id(0) == 0)
        def _():
            dw_ref[...] = rest[0][...] if totals else jnp.zeros_like(dw_ref)
            dg_ref[...] = rest[1][...] if totals else jnp.zeros_like(dg_ref)

        dw_ref[...] += dw
        dg_ref[0:8, :] += dgh
        dg_ref[8:16, :] += dge
        dg_ref[16:24, :] += dgf

    cols = pl.BlockSpec((width, tile), lambda i: (0, i))
    sums = [pl.BlockSpec((width, 2 * width), lambda i: (0, 0)), pl.BlockSpec((24, width), lambda i: (0, 0))]
    return pl.pallas_call(
        body,
        grid=(n // tile,),
        in_specs=tiles_of(tile, width, width, width) + [
            pl.BlockSpec((width, 2 * width), lambda i: (0, 0)), pl.BlockSpec((3, width), lambda i: (0, 0)), cols, cols]
        + sums[:len(totals)],
        out_specs=tiles_of(tile, width, width) + sums,
        out_shape=[
            jax.ShapeDtypeStruct((n, width), bf16), jax.ShapeDtypeStruct((n, width), f32),
            jax.ShapeDtypeStruct((width, 2 * width), f32), jax.ShapeDtypeStruct((24, width), f32)],
        compiler_params=params(),
        cost_estimate=pl.CostEstimate(flops=12 * n * width * width, bytes_accessed=24 * n * width, transcendentals=3 * n),
        name="back",
    )(hid, own, recv, w_proj, gains, df_mine, df_recv, *totals)


def merge_stats(mine, other, swap_halves, wt):
    n = mine.shape[1]

    def body(a_ref, b_ref, *rest):
        m, s = a_ref[0:1, :], a_ref[1:2, :]
        if swap_halves:
            b = jnp.concatenate([b_ref[:, n // 2:], b_ref[:, :n // 2]], axis=1)
        else:
            b = b_ref[...]
        top = jnp.maximum(m, b[0:1, :])
        total = s * jnp.exp2(m - top) + b[1:2, :] * jnp.exp2(b[0:1, :] - top)
        if wt is None:
            rest[0][...] = jnp.concatenate([top, total], axis=0)
        else:
            lse = top + jnp.log2(total)
            rest[1][...] = lse
            rest[2][...] = lse - jnp.log2(rest[0][...])

    row = jax.ShapeDtypeStruct((1, n), f32)
    args = (mine, other) if wt is None else (mine, other, wt)
    return pl.pallas_call(
        body,
        out_shape=jax.ShapeDtypeStruct((2, n), f32) if wt is None else [row, row],
        name="merge_stats",
    )(*args)


def round_rows(parts):
    m, (n, width) = len(parts), parts[0].shape
    tile = 768
    steps = n // tile

    def body(*refs):
        k = pl.program_id(0)
        for i in range(m):
            @pl.when(k == i)
            def _(i=i):
                refs[m][...] = refs[i][...].astype(bf16)

    def spec(i):
        return pl.BlockSpec((tile, width), lambda k, b: (jnp.where(k == i, b, jnp.where(k > i, steps - 1, 0)), 0))

    return pl.pallas_call(
        body,
        grid=(m, steps),
        in_specs=[spec(i) for i in range(m)],
        out_specs=pl.BlockSpec((tile, width), lambda k, b: (k * steps + b, 0)),
        out_shape=jax.ShapeDtypeStruct((m * n, width), bf16),
        compiler_params=params(),
        name="round_rows",
    )(*parts)


def logits_kernel(core, out_tab, feats, rows):
    n = feats.shape[0]
    t, lanes, groups = 768, 256, 2
    nv, nj = rows // V_TILE, n // (2 * t)

    def stats(y_ref, m_ref, s_ref, start):
        for l in range(0, t, lanes):
            sl = pl.ds(pl.multiple_of(start + l, lanes), lanes)
            old = m_ref[:, sl]
            acc = [old] + [None] * (groups - 1)
            for i, r in enumerate(range(0, V_TILE, 8)):
                x = y_ref[r:r + 8, l:l + lanes]
                acc[i % groups] = x if acc[i % groups] is None else jnp.maximum(acc[i % groups], x)
            new = tree(jnp.maximum, acc)
            acc = [s_ref[:, sl] * jnp.exp2(old - new)] + [None] * (groups - 1)
            for i, r in enumerate(range(0, V_TILE, 8)):
                x = jnp.exp2(y_ref[r:r + 8, l:l + lanes] - new)
                acc[i % groups] = x if acc[i % groups] is None else acc[i % groups] + x
            s_ref[:, sl] = tree(jnp.add, acc)
            m_ref[:, sl] = new

    def body(core_ref, w_ref, f_ref, y_ref, st_ref, ya, yb, m_ref, s_ref):
        v, j = pl.program_id(0), pl.program_id(1)
        step = v * nj + j

        @pl.when(step == 0)
        def _():
            m_ref[...] = jnp.full_like(m_ref, NEG)
            s_ref[...] = jnp.zeros_like(s_ref)
            yb[...] = jnp.full_like(yb, 2 * NEG)

        base = pl.multiple_of(j * 2 * t, 2 * t)
        prev = pl.multiple_of(lax.rem(j + nj - 1, nj) * 2 * t, 2 * t)
        w = w_ref[...]

        def dot(start, buf, lo):
            y = lax.dot_general(w, f_ref[pl.ds(start, t), :], NT, preferred_element_type=f32) * LOG2E
            buf[...] = y
            y_ref[:, lo:lo + t] = y

        dot(base, ya, 0)
        stats(yb, m_ref, s_ref, prev + t)
        dot(base + t, yb, t)
        stats(ya, m_ref, s_ref, base)

        @pl.when(step == nv * nj - 1)
        def _():
            stats(yb, m_ref, s_ref, base + t)
            m = m_ref[...]
            top = jnp.max(m, axis=0, keepdims=True)
            st_ref[0:1, :] = top
            st_ref[1:2, :] = jnp.sum(s_ref[...] * jnp.exp2(m - top), axis=0, keepdims=True)

    grid_spec = pltpu.PrefetchScalarGridSpec(
        num_scalar_prefetch=1,
        grid=(nv, nj),
        in_specs=[
            pl.BlockSpec((V_TILE, 512), lambda v, j, c: (c[0] * nv + v, 0)),
            pl.BlockSpec((n, 512), lambda v, j, c: (0, 0), **once()),
        ],
        out_specs=[pl.BlockSpec((V_TILE, 2 * t), lambda v, j, c: (v, j)), pl.BlockSpec((2, n), lambda v, j, c: (0, 0))],
        scratch_shapes=[pltpu.VMEM((V_TILE, t), f32)] * 2 + [pltpu.VMEM((8, n), f32)] * 2,
    )
    return pl.pallas_call(
        body,
        grid_spec=grid_spec,
        out_shape=[jax.ShapeDtypeStruct((rows, n), f32), jax.ShapeDtypeStruct((2, n), f32)],
        compiler_params=params(),
        cost_estimate=cost(1, rows, n, 4 * rows * n),
        name="logits",
    )(core, out_tab, feats)


def own_kernel(core, logits, feats, out_tab, lab, le, wt, acc):
    rows, n = logits.shape
    t, lanes, pm, pn, pr = 768, 256, 12, 256, 8
    nv, nj = rows // V_TILE, n // t
    last = nv * nj

    def body(core_ref, y_ref, f_ref, w_ref, lab_ref, le_ref, wt_ref, *rest):
        if acc is not None:
            in_ref, dw_ref, dfa_ref, dfb_ref, hit_ref, ga, gb, df_ref = rest
        else:
            dw_ref, dfa_ref, dfb_ref, hit_ref, ga, gb, df_ref = rest
        s = pl.program_id(0)
        v, j, pj = s // nj, lax.rem(s, nj), lax.rem(s - 1 + nj, nj)
        base, prev = pl.multiple_of(j * t, t), pl.multiple_of(pj * t, t)
        half = pj // (nj // 2)
        half_start = (pj - half * (nj // 2)) * t

        @pl.when(s == 0)
        def _():
            df_ref[...] = jnp.zeros_like(df_ref)
            hit_ref[...] = jnp.zeros_like(hit_ref)

        @pl.when((pj == 0) & (s > 0))
        def _():
            dw_ref[...] = jnp.zeros_like(dw_ref) if acc is None else in_ref[...]

        def grads(g):
            return [
                functools.partial(grad_piece, y_ref, g, lab_ref, le_ref, wt_ref, hit_ref, base, v * V_TILE, lanes, False, l, r0, r1)
                for l in range(0, t, lanes) for r0, r1 in cuts(V_TILE, pr, 16)
            ]

        def dots(g):
            def out_piece(r0, r1):
                dw_ref[r0:r1, :] += lax.dot_general(g[r0:r1, :], f_ref[pl.ds(prev, t), :], NN, preferred_element_type=f32)

            def feat_piece(l):
                sl = pl.ds(pl.multiple_of(half_start + l, pn), pn)
                df_ref[half, :, sl] += lax.dot_general(w_ref[...], g[:, l:l + pn], TN, preferred_element_type=f32)

            return alternate(
                [functools.partial(out_piece, r0, r1) for r0, r1 in cuts(V_TILE, pm, 16)],
                [functools.partial(feat_piece, l) for l in range(0, t, pn)],
            )

        odd = lax.rem(s, 2) == 1

        @pl.when(s == 0)
        def _():
            interleave([], grads(ga))

        @pl.when((s > 0) & (s < last) & odd)
        def _():
            interleave(dots(ga), grads(gb))

        @pl.when((s > 0) & (s < last) & jnp.logical_not(odd))
        def _():
            interleave(dots(gb), grads(ga))

        @pl.when(s == last)
        def _():
            interleave(dots(ga if last % 2 == 1 else gb), [])
            dfa_ref[...] = df_ref[0]
            dfb_ref[...] = df_ref[1]

    def now(s):
        return jnp.minimum(s, last - 1)

    def lag(s):
        return jnp.maximum(s - 1, 0) // nj

    row = pl.BlockSpec((1, n), lambda s, c: (0, 0), **once())
    in_specs = [
        pl.BlockSpec((V_TILE, t), lambda s, c: (now(s) // nj, lax.rem(now(s), nj))),
        pl.BlockSpec((n, 512), lambda s, c: (0, 0), **once()),
        pl.BlockSpec((V_TILE, 512), lambda s, c: (c[0] * nv + lag(s), 0)),
        row, row, row,
    ]
    args = [logits, feats, out_tab, lab, le, wt]
    if acc is not None:
        in_specs.append(pl.BlockSpec((V_TILE, 512), lambda s, c: (lag(s), 0)))
        args.append(acc)
    grid_spec = pltpu.PrefetchScalarGridSpec(
        num_scalar_prefetch=1,
        grid=(last + 1,),
        in_specs=in_specs,
        out_specs=[
            pl.BlockSpec((V_TILE, 512), lambda s, c: (lag(s), 0)),
            pl.BlockSpec((512, n // 2), lambda s, c: (0, 0), **once()),
            pl.BlockSpec((512, n // 2), lambda s, c: (0, 0), **once()),
            pl.BlockSpec((16, n), lambda s, c: (0, 0), **once()),
        ],
        scratch_shapes=[pltpu.VMEM((V_TILE, t), bf16)] * 2 + [pltpu.VMEM((2, 512, n // 2), f32)],
    )
    return pl.pallas_call(
        body,
        grid_spec=grid_spec,
        out_shape=[
            jax.ShapeDtypeStruct((rows, 512), f32), jax.ShapeDtypeStruct((512, n // 2), f32),
            jax.ShapeDtypeStruct((512, n // 2), f32), jax.ShapeDtypeStruct((16, n), f32)],
        input_output_aliases={7: 0} if acc is not None else {},
        compiler_params=params(),
        cost_estimate=cost(2, rows, n, 4 * rows * n),
        name="own",
    )(core, *args)


def other_kernel(core, feats, out_tab, lab, le, wt, acc, whole, part):
    n = feats.shape[0]
    rows = acc.shape[0]
    t, lanes, pz, pm, pr = 768, 256, 6, 6, 4
    nv_all = rows // V_TILE
    nv, nj = nv_all // N_PART, n // t
    v0 = part * nv
    last = nv * nj

    def body(core_ref, f_ref, w_ref, lab_ref, le_ref, wt_ref, in_ref, *rest):
        if whole is not None:
            rest = rest[1:]
        part_ref, dw_ref, ya, yb, ga, gb = rest
        s = pl.program_id(0)

        def start(k):
            return pl.multiple_of(lax.rem(s - k + 2 * nj, nj) * t, t)

        b0, b1, b2 = start(0), start(1), start(2)
        row0 = jnp.where(s >= 1, (v0 + (s - 1) // nj) * V_TILE, 1 << 24)

        @pl.when(s == 0)
        def _():
            yb[...] = jnp.full_like(yb, NEG)
            ga[...] = jnp.zeros_like(ga)
            gb[...] = jnp.zeros_like(gb)

        @pl.when((b2 == 0) & (s > 1))
        def _():
            dw_ref[...] = in_ref[...]

        def step(y_new, y_old, g_new, g_old):
            def logit_piece(r0, r1):
                y_new[r0:r1, :] = lax.dot_general(w_ref[r0:r1, :], f_ref[pl.ds(b0, t), :], NT, preferred_element_type=f32)

            def out_piece(r0, r1):
                dw_ref[r0:r1, :] += lax.dot_general(g_old[r0:r1, :], f_ref[pl.ds(b2, t), :], NN, preferred_element_type=f32)

            dots = alternate(
                [functools.partial(logit_piece, r0, r1) for r0, r1 in cuts(V_TILE, pz, 16)],
                [functools.partial(out_piece, r0, r1) for r0, r1 in cuts(V_TILE, pm, 16)],
            )
            grads = [
                functools.partial(grad_piece, y_old, g_new, lab_ref, le_ref, wt_ref, None, b1, row0, lanes, True, l, r0, r1)
                for l in range(0, t, lanes) for r0, r1 in cuts(V_TILE, pr, 16)
            ]
            interleave(dots, grads)

        odd = lax.rem(s, 2) == 1

        @pl.when(odd)
        def _():
            step(yb, ya, ga, gb)

        @pl.when(jnp.logical_not(odd))
        def _():
            step(ya, yb, gb, ga)

        @pl.when((lax.rem(s - 2 + nj, nj) == nj - 1) & (s > 1))
        def _():
            part_ref[...] = dw_ref[...]

    def now(s):
        return v0 + jnp.minimum(s, last - 1) // nj

    def lag(s):
        return jnp.maximum(s - 2, 0) // nj

    row = pl.BlockSpec((1, n), lambda s, c: (0, 0), **once())
    in_specs = [
        pl.BlockSpec((n, 512), lambda s, c: (0, 0), **once()),
        pl.BlockSpec((V_TILE, 512), lambda s, c: (c[0] * nv_all + now(s), 0)),
        row, row, row,
        pl.BlockSpec((V_TILE, 512), lambda s, c: (v0 + lag(s), 0)),
    ]
    args = [feats, out_tab, lab, le, wt, acc]
    if whole is not None:
        in_specs.append(pl.BlockSpec(memory_space=pl.ANY))
        args.append(whole)
    grid_spec = pltpu.PrefetchScalarGridSpec(
        num_scalar_prefetch=1,
        grid=(last + 2,),
        in_specs=in_specs,
        out_specs=[
            pl.BlockSpec((V_TILE, 512), lambda s, c: (lag(s), 0)),
            pl.BlockSpec((V_TILE, 512), lambda s, c: (c[0] * nv_all + v0 + lag(s), 0)),
        ],
        scratch_shapes=[pltpu.VMEM((V_TILE, t), f32)] * 2 + [pltpu.VMEM((V_TILE, t), bf16)] * 2,
    )
    return pl.pallas_call(
        body,
        grid_spec=grid_spec,
        out_shape=[jax.ShapeDtypeStruct((nv * V_TILE, 512), f32), jax.ShapeDtypeStruct((2 * rows, 512), f32)],
        input_output_aliases={7: 1} if whole is not None else {},
        compiler_params=params(),
        cost_estimate=cost(2, nv * V_TILE, n, 12 * nv * V_TILE * 512),
        name="other",
    )(core, *args)


def row_sums(order, ids, bounds, parts, block):
    m, (n, width) = len(parts), parts[0].shape
    unroll = 16

    def body(order_ref, id_ref, b_ref, *rest):
        ins, (out_ref, buf, sem) = rest[:m], rest[m:]
        p = pl.program_id(0)

        def fetch(i):
            return pltpu.make_async_copy(ins[i], buf.at[pl.ds(i * n, n)], sem.at[i])

        @pl.when(p == 0)
        def _():
            for i in range(m):
                fetch(i).start()

        out_ref[...] = jnp.zeros_like(out_ref)

        @pl.when(p == 0)
        def _():
            for i in range(m):
                fetch(i).wait()

        lo, hi = b_ref[p], b_ref[p + 1]

        def one(k, carry):
            prev, acc = carry
            row, d = order_ref[k], id_ref[k]
            x = buf[pl.ds(row, 1), :]
            acc = jnp.where(d == prev, acc + x, x)
            out_ref[pl.ds(d - p * V_TILE, 1), :] = acc
            return d, acc

        def several(i, carry):
            for u in range(unroll):
                carry = one(lo + i * unroll + u, carry)
            return carry

        full = (hi - lo) // unroll
        carry = lax.fori_loop(0, full, several, (jnp.int32(-1), jnp.zeros((1, width), f32)))
        lax.fori_loop(lo + full * unroll, hi, one, carry)

    grid_spec = pltpu.PrefetchScalarGridSpec(
        num_scalar_prefetch=3,
        grid=(block // V_TILE,),
        in_specs=[pl.BlockSpec(memory_space=pl.ANY)] * m,
        out_specs=pl.BlockSpec((V_TILE, width), lambda p, *_: (p, 0)),
        scratch_shapes=[pltpu.VMEM((m * n, width), f32), pltpu.SemaphoreType.DMA((m,))],
    )
    return pl.pallas_call(
        body,
        grid_spec=grid_spec,
        out_shape=jax.ShapeDtypeStruct((block, width), f32),
        compiler_params=params(),
        cost_estimate=pl.CostEstimate(flops=150_000_000, bytes_accessed=4 * (m * n + block) * width, transcendentals=0),
        name="row_sums",
    )(order, ids, bounds, *parts)


def solution(mesh):
    def local_step(hidden, tokens, emb_blk, out_blk, w_proj, gain_h, gain_e, gain_f):
        batch, piece, width = hidden.shape
        block = emb_blk.shape[0]
        rows = block // 2
        n_own = batch * piece
        n_c = n_own // N_CHUNK
        tp_rank, cp_rank = lax.axis_index("tp"), lax.axis_index("cp")
        core = lax.rem(cp_rank, 2)
        core_arg = core.reshape(1)
        seq_len = piece * 4
        row_start = tp_rank * block + core * rows

        def core_swap(v):
            return lax.ppermute(v, "cp", CORE_SWAP)

        def x_swap(v):
            return lax.ppermute(v, "cp", X_SWAP)

        def y_swap(v):
            return lax.ppermute(v, "tp", Y_SWAP)

        def weight_of(rank):
            pos = rank * piece + jnp.arange(piece)
            return jnp.broadcast_to(MTP_WEIGHT * (pos < seq_len - 2).astype(f32), (batch, piece)).reshape(N_CHUNK, n_c)

        head = lax.ppermute(tokens[:, :2], "cp", [(k + 1, k) for k in range(3)])
        ahead = jnp.concatenate([tokens, head], axis=1)
        ids_own = jnp.stack([ahead[:, 1:piece + 1], ahead[:, 2:]]).reshape(2, N_CHUNK, n_c)
        ids_mate = core_swap(ids_own)
        ids_far = x_swap(ids_own)
        ids_diag = core_swap(ids_far)
        next_ids = [v[0] for v in (ids_own, ids_mate, ids_far, ids_diag)]
        labels = [v[1] - row_start for v in (ids_own, ids_mate, ids_far, ids_diag)]
        weights = [weight_of(cp_rank ^ k) for k in range(4)]

        local_next = next_ids[0] - tp_rank * block
        in_block = (local_next >= 0) & (local_next < block)
        take = jnp.clip(local_next, 0, block - 1)
        hid = hidden.reshape(N_CHUNK, n_c, width)

        emb_own, emb_recv = [], []
        for c in range(N_CHUNK):
            e = jnp.where(in_block[c][:, None], jnp.take(emb_blk, take[c], axis=0).astype(f32), 0.0)
            emb_own.append(e)
            emb_recv.append(y_swap(e))

        ids_all = jnp.concatenate([next_ids[k].reshape(-1) for k in (0, 2, 1, 3)]) - tp_rank * block
        seg = jnp.where((ids_all >= 0) & (ids_all < block), ids_all, block)
        seg_sorted, order = lax.sort((seg, jnp.arange(4 * n_own, dtype=jnp.int32)), num_keys=1)
        starts = jnp.arange(block // V_TILE + 1) * V_TILE
        bounds = jnp.sum(seg[None, :] < starts[:, None], axis=1).astype(jnp.int32)

        gains = jnp.stack([gain_h, gain_e, gain_f])
        f_pair, far_parts, logits, stats = [], [], [], []
        for c in range(N_CHUNK):
            normed = front_kernel(hid[c], emb_own[c], emb_recv[c], w_proj, gains)
            mate = core_swap(normed)
            f_pair.append(round_rows([normed, mate]))
            far = x_swap(normed)
            far_parts += [far, core_swap(far)]
            y, st = logits_kernel(core_arg, out_blk, f_pair[c], rows)
            logits.append(y)
            stats.append(st)

        le_pair, le_far, lse_own, wt_pair = [], [], [], []
        for c in range(N_CHUNK):
            recv = core_swap(stats[c])
            both = merge_stats(stats[c], recv, True, None)
            recv = y_swap(both)
            wt_pair.append(jnp.concatenate([weights[0][c], weights[1][c]])[None])
            lse, le = merge_stats(both, recv, False, wt_pair[c])
            lse_own.append(lse[0, :n_c])
            le_pair.append(le)
            le_far.append(x_swap(le))

        acc, df_terms, hits = None, [], []
        for c in range(N_CHUNK):
            lab = jnp.concatenate([labels[0][c], labels[1][c]])
            acc, df_own, df_mate, hit = own_kernel(core_arg, logits[c], f_pair[c], out_blk, lab[None], le_pair[c], wt_pair[c], acc)
            recv = core_swap(df_mate)
            mine = df_own + recv
            recv = y_swap(mine)
            df_terms.append((mine, recv))
            hits.append(hit)

        f_far = round_rows(far_parts)
        lab_far = jnp.concatenate([labels[k][c] for c in range(N_CHUNK) for k in (2, 3)])
        wt_far = jnp.concatenate([weights[k][c] for c in range(N_CHUNK) for k in (2, 3)])
        whole, mates = None, []
        for part in range(N_PART):
            piece_out, whole = other_kernel(core_arg, f_far, out_blk, lab_far[None], jnp.concatenate(le_far, axis=1), wt_far[None], acc, whole, part)
            mates.append(core_swap(piece_out))

        d_hid, totals, de_own, de_far, de_mate, de_diag = [], (), [], [], [], []
        for c in range(N_CHUNK):
            dh, de, *totals = back_kernel(hid[c], emb_own[c], emb_recv[c], w_proj, gains, *df_terms[c], totals)
            d_hid.append(dh)
            de_own.append(de)
            de_far.append(x_swap(de))
            de_mate.append(core_swap(de))
            de_diag.append(core_swap(de_far[c]))

        loss_part = 0.5 * jnp.sum(weights[0] * jnp.stack(lse_own)) - sum(jnp.sum(w * h) for w, h in zip(wt_pair, hits))
        d_proj = totals[0]
        small = jnp.concatenate([jnp.sum(totals[1].reshape(3, 8, width), axis=1), jnp.full((5, width), loss_part)], axis=0)
        d_proj, small = d_proj + core_swap(d_proj), small + core_swap(small)
        d_proj, small = d_proj + x_swap(d_proj), small + x_swap(small)
        loss_sum = small[3:4, 0] + y_swap(small[3:, :128])[0:1, 0]

        d_emb = row_sums(order, seg_sorted, bounds, de_own + de_far + de_mate + de_diag, block)

        for part in range(N_PART):
            start = (1 - core) * rows + part * (rows // N_PART)
            whole = lax.dynamic_update_slice(whole, mates[part], (start, 0))

        loss = LN2 * loss_sum / (batch * (seq_len - 2))
        d_hidden = jnp.concatenate(d_hid, axis=0).reshape(batch, piece, width)
        return loss, d_hidden, d_proj, d_emb, whole, small[0], small[1], small[2]

    part_seq = P("dp", "cp", None)
    in_specs = (part_seq, P("dp", "cp"), P("tp", None), P("tp", None), P(None, None), P(None), P(None), P(None))
    out_specs = (P("dp"), part_seq, P("dp", None), P(("dp", "tp"), None), P(("dp", "tp"), None), P("dp"), P("dp"), P("dp"))
    return jax.shard_map(local_step, mesh=mesh, in_specs=in_specs, out_specs=out_specs, check_vma=False)
```

time: 3080 us -> 1740 us (0.56)
  waiting for transfers between devices: 1990 us -> 469 us
  Pallas kernels: 0 us -> 1070 us
  matrix products: 455 us -> 0 us
  other arithmetic: 487 us -> 55 us
  starting transfers between devices: 2.2 us -> 33.5 us
    psum x3 -> x0, waiting for transfers between devices: 1990 us -> none  [the longest x1 1700 us: local_step(): lax.psum((d_out, d_emb, d_proj, d_gain_h, d_gain_e, d_gain_f, loss_part),...]
    pallas_call x0 -> x26, Pallas kernels: none -> 1070 us  [the longest x3 335 us: own_kernel(): pl.pallas_call(body, grid_spec=grid_spec, out_shape=[jax.ShapeDtypeStruct...]
    ppermute x1 -> x48, waiting for transfers between devices: 3.94 us -> 469 us  [the longest x12 231 us: x_swap(): return lax.ppermute(v, 'cp', X_SWAP)]
    dot_general x6 -> x0, matrix products: 455 us -> none  [the longest x1 159 us: local_step(): jnp.einsum('bsd,vd->bsv', features, out_blk, preferred_element_type=jnp.f...]
    convert_element_type x5 -> x0, other arithmetic: 229 us -> none  [the longest x1 219 us: local_step(): (MTP_WEIGHT * pos_weight[:, None] * (soft_prob - is_label.astype(jnp.floa...]
    reduce_sum x6 -> x4, other arithmetic: 183 us -> 4.97 us  [the longest x1 1.86 us: local_step(): jnp.sum(w * h)]
    unnamed x77 -> x56, local copies, waits for them, and re-layouts: 82.8 us -> 11.8 us
    scatter-add x1 -> x0, other arithmetic: 49 us -> none  [local_step(): jax.ops.segment_sum(d_embrow.reshape(-1, width), seg_ids, num_segments=vo...]
  transfers between devices with their start and end apart: 4 -> 48, of which waited for: 4 -> 14; matrix products, arithmetic and copies ran while one was open for 5% -> 8% of each run, Pallas kernels for 0% -> 54%
where the time goes in v1:
time: 1740 us; the launch traced here: 1730 us
  Pallas kernels  1070 us (61%)
  waiting for transfers between devices  469 us (27%)
  local copies, waits for them, and re-layouts  104 us (6%)
  other arithmetic  55 us (3%)
  starting transfers between devices  33.5 us (2%)
    pallas_call x3, Pallas kernels, own_kernel(): pl.pallas_call(body, grid_spec=grid_spec, out_shape=[jax.ShapeDtypeStruct...  335 us
    pallas_call x3, Pallas kernels, other_kernel(): pl.pallas_call(body, grid_spec=grid_spec, out_shape=[jax.ShapeDtypeStruct...  329 us
    ppermute x12, waiting for transfers between devices, x_swap(): return lax.ppermute(v, 'cp', X_SWAP)  231 us
    ppermute x10, waiting for transfers between devices, y_swap(): return lax.ppermute(v, 'tp', Y_SWAP)  198 us
    pallas_call x3, Pallas kernels, logits_kernel(): pl.pallas_call(body, grid_spec=grid_spec, out_shape=[jax.ShapeDtypeStruct...  188 us
    pallas_call x1, Pallas kernels, row_sums(): pl.pallas_call(body, grid_spec=grid_spec, out_shape=jax.ShapeDtypeStruct(...  108 us
    gather x3, local copies, waits for them, and re-layouts, local_step(): jnp.take(emb_blk, take[c], axis=0).astype(f32)  51.5 us
    pallas_call x3, Pallas kernels, back_kernel(): pl.pallas_call(body, grid=(n // tile,), in_specs=tiles_of(tile, width, wi...  43.1 us
  transfers between devices with their start and end apart: 48, of which 14 were waited for; matrix products, arithmetic and copies ran while one was open for 8% of the time, Pallas kernels for 54%

profile of v1, /device:TPU:1, one launch (start us, length us, event | category | flops | bytes accessed | tf_op | source)
XLA Modules:
  0.0 1733.9 jit_solution(10282636429713871971)
XLA Ops:
  1.3 1.9 collective-permute-start
  3.8 3.4 collective-permute-done
  8.3 17.3 gather_fusion
  25.6 2.5 convert_select_fusion.2.own_ref
  30.1 4.6 fusion.1
  36.5 17.1 gather_fusion.2
  53.6 17.1 gather_fusion.1
  70.8 3.8 convert_select_fusion.own_ref
  75.0 2.6 convert_select_fusion.1.own_ref
  79.2 19.2 %collective-permute-done.1.recv_ref = f32[1536,512]{1,0:T(8,128)} collective-permute-done((f32[1536,512]{1,0:T(8,128)S(1)}, f32[1536,512]{1,0:T(8,128)}, u32[]{:S(2)}, u32[]{:S(2)}) %collective-permute-start.1) | collective-permute-done | bytes 3145760 | tf_op jit(solution)/shard_map/ppermute | solution.py:597
  98.4 7.8 front.3.refs_0_
  106.2 1.3 constant_dynamic-update-slice_fusion
  123.2 108.3 %collective-permute-done.6.recv_ref = f32[1536,512]{1,0:T(8,128)} collective-permute-done((f32[1536,512]{1,0:T(8,128)}, f32[1536,512]{1,0:T(8,128)}, u32[]{:S(2)}, u32[]{:S(2)}) %collective-permute-start.6) | collective-permute-done | bytes 3145760 | tf_op jit(solution)/shard_map/ppermute | solution.py:597
  231.6 7.6 front.4.refs_0_
  239.3 1.7 collective-permute-start.7
  241.0 7.6 front.5.refs_0_
  249.0 1.4 collective-permute-start.40
  250.4 5.5 round_rows.4.f_ref
  255.9 62.5 %logits.3 = (f32[12576,3072]{1,0:T(8,128)}, f32[2,3072]{1,0:T(2,128)}) custom-call(s32[1]{0:T(128)} %bitcast.4.core_ref, bf16[25152,512]{1,0:T(8,128)(2,1)} %w_ref.29, bf16[3072,512]{1,0:T(8,128)(2,1)} %round_rows.4.f_ref), custom_call_target="tpu_custom_call" | custom-call | flops 39560675328 | bytes 154533888 | tf_op jit(solution)/shard_map/logits/pallas_call | solution.py:301
  318.9 5.5 round_rows.6.f_ref
  324.4 62.8 %logits.5 = (f32[12576,3072]{1,0:T(8,128)}, f32[2,3072]{1,0:T(2,128)}) custom-call(s32[1]{0:T(128)} %bitcast.4.core_ref, bf16[25152,512]{1,0:T(8,128)(2,1)} %w_ref.29, bf16[3072,512]{1,0:T(8,128)(2,1)} %round_rows.6.f_ref), custom_call_target="tpu_custom_call" | custom-call | flops 39560675328 | bytes 154533888 | tf_op jit(solution)/shard_map/logits/pallas_call | solution.py:301
  387.3 5.5 round_rows.5.f_ref
  392.9 62.3 %logits.4 = (f32[12576,3072]{1,0:T(8,128)}, f32[2,3072]{1,0:T(2,128)}) custom-call(s32[1]{0:T(128)} %bitcast.4.core_ref, bf16[25152,512]{1,0:T(8,128)(2,1)} %w_ref.29, bf16[3072,512]{1,0:T(8,128)(2,1)} %round_rows.5.f_ref), custom_call_target="tpu_custom_call" | custom-call | flops 39560675328 | bytes 154533888 | tf_op jit(solution)/shard_map/logits/pallas_call | solution.py:301
  455.6 1.4 merge_stats.10.a_ref
  460.5 1.4 merge_stats.6.a_ref
  462.5 1.4 merge_stats.8.a_ref
  464.8 1.4 merge_stats.11
  466.2 108.6 %own.3 = (f32[12576,512]{1,0:T(8,128)}, f32[512,1536]{1,0:T(8,128)}, f32[512,1536]{1,0:T(8,128)}, f32[16,3072]{1,0:T(8,128)}) custom-call(s32[1]{0:T(128)} %bitcast.4.core_ref, f32[12576,3072]{1,0:T(8,128)} %get-tuple-element.59.y_ref, bf16[3072,512]{1,0:T(8,128)(2,1)} %round_rows.6.f_ref, bf16[25152,512]{1,0:T(8,128)(2,1)} %w_ref.29, s32[1,3072]{1,0:T(1,128)} %bitcast.35, ...), custom_call_target="tpu_custom_call" | custom-call | flops 79121350656 | bytes 154533888 | tf_op jit(solution)/shard_map/own/pallas_call | solution.py:405
  575.4 1.4 merge_stats.7
  577.7 1.4 merge_stats.9
  579.1 113.3 %own.4 = (f32[12576,512]{1,0:T(8,128)}, f32[512,1536]{1,0:T(8,128)}, f32[512,1536]{1,0:T(8,128)}, f32[16,3072]{1,0:T(8,128)}) custom-call(s32[1]{0:T(128)} %bitcast.4.core_ref, f32[12576,3072]{1,0:T(8,128)} %get-tuple-element.56.y_ref, bf16[3072,512]{1,0:T(8,128)(2,1)} %round_rows.5.f_ref, ...), custom_call_target="tpu_custom_call", output_to_operand_aliasing={{0}: (7, {})} | custom-call | flops 79121350656 | bytes 154533888 | tf_op jit(solution)/shard_map/own/pallas_call | solution.py:405
  692.5 113.3 %own.5 = (f32[12576,512]{1,0:T(8,128)}, f32[512,1536]{1,0:T(8,128)}, f32[512,1536]{1,0:T(8,128)}, f32[16,3072]{1,0:T(8,128)}) custom-call(s32[1]{0:T(128)} %bitcast.4.core_ref, f32[12576,3072]{1,0:T(8,128)} %get-tuple-element.53.y_ref, bf16[3072,512]{1,0:T(8,128)(2,1)} %round_rows.4.f_ref, ...), custom_call_target="tpu_custom_call", output_to_operand_aliasing={{0}: (7, {})} | custom-call | flops 79121350656 | bytes 154533888 | tf_op jit(solution)/shard_map/own/pallas_call | solution.py:405
  807.8 1.9 multiply_reduce_fusion
  816.4 2.7 collective-permute-start.18
  821.5 15.8 round_rows.7.f_ref
  837.3 109.0 %other.3 = (f32[4192,512]{1,0:T(8,128)}, f32[25152,512]{1,0:T(8,128)}) custom-call(s32[1]{0:T(128)} %bitcast.4.core_ref, bf16[9216,512]{1,0:T(8,128)(2,1)} %round_rows.7.f_ref, bf16[25152,512]{1,0:T(8,128)(2,1)} %w_ref.29, s32[1,9216]{1,0:T(1,128)} %bitcast.42, f32[1,9216]{1,0:T(1,128)} %constant_dynamic-update-slice_fusion.4.le_ref, f32[1,9216]{1,0:T(1,128)} %bitcast.45, ...), custom_call_target="tpu_custom_call" | custom-call | flops 79121350656 | bytes 25755648 | tf_op jit(solution)/shard_map/other/pallas_call | solution.py:507
  946.4 5.3 add.92.a_ref
  952.0 4.4 add.90.a_ref
  957.6 4.1 add.91.a_ref
  962.0 110.1 %other.4 = (f32[4192,512]{1,0:T(8,128)}, f32[25152,512]{1,0:T(8,128)}) custom-call(s32[1]{0:T(128)} %bitcast.4.core_ref, bf16[9216,512]{1,0:T(8,128)(2,1)} %round_rows.7.f_ref, bf16[25152,512]{1,0:T(8,128)(2,1)} %w_ref.29, s32[1,9216]{1,0:T(1,128)} %bitcast.43, ...), custom_call_target="tpu_custom_call", output_to_operand_aliasing={{1}: (7, {})} | custom-call | flops 79121350656 | bytes 25755648 | tf_op jit(solution)/shard_map/other/pallas_call | solution.py:507
  1072.0 13.9 back.3
  1086.0 70.5 %collective-permute-done.17.b_ref = f32[512,1536]{1,0:T(8,128)} collective-permute-done((f32[512,1536]{1,0:T(8,128)}, f32[512,1536]{1,0:T(8,128)}, u32[]{:S(2)}, u32[]{:S(2)}) %collective-permute-start.17) | collective-permute-done | bytes 3145760 | tf_op jit(solution)/shard_map/ppermute | solution.py:597
  1156.5 14.7 back.4
  1171.2 14.5 back.5
  1188.6 109.8 %other.5 = (f32[4192,512]{1,0:T(8,128)}, f32[25152,512]{1,0:T(8,128)}) custom-call(s32[1]{0:T(128)} %bitcast.4.core_ref, bf16[9216,512]{1,0:T(8,128)(2,1)} %round_rows.7.f_ref, bf16[25152,512]{1,0:T(8,128)(2,1)} %w_ref.29, s32[1,9216]{1,0:T(1,128)} %bitcast.44, ...), custom_call_target="tpu_custom_call", output_to_operand_aliasing={{1}: (7, {})} | custom-call | flops 79121350656 | bytes 25755648 | tf_op jit(solution)/shard_map/other/pallas_call | solution.py:507
  1300.1 2.2 collective-permute-done.21
  1302.6 1.9 collective-permute-start.23
  1304.8 2.7 collective-permute-start.30
  1307.5 32.1 %collective-permute-done.23 = f32[512,1024]{1,0:T(8,128)S(1)} collective-permute-done((f32[512,1024]{1,0:T(8,128)}, f32[512,1024]{1,0:T(8,128)S(1)}, u32[]{:S(2)}, u32[]{:S(2)}) %collective-permute-start.23) | collective-permute-done | bytes 2097184 | tf_op jit(solution)/shard_map/ppermute | solution.py:591
  1340.0 4.1 collective-permute-done.30.rest_6_
  1344.5 64.9 %collective-permute-done.27.rest_3_ = f32[1536,512]{1,0:T(8,128)S(1)} collective-permute-done((f32[1536,512]{1,0:T(8,128)}, f32[1536,512]{1,0:T(8,128)S(1)}, u32[]{:S(2)}, u32[]{:S(2)}) %collective-permute-start.27) | collective-permute-done | bytes 3145760 | tf_op jit(solution)/shard_map/ppermute | solution.py:594
  1409.3 1.7 copy-done.3
  1411.4 2.0 add.98
  1413.4 63.4 %collective-permute-done.29.rest_5_ = f32[1536,512]{1,0:T(8,128)} collective-permute-done((f32[1536,512]{1,0:T(8,128)}, f32[1536,512]{1,0:T(8,128)}, u32[]{:S(2)}, u32[]{:S(2)}) %collective-permute-start.29) | collective-permute-done | bytes 3145760 | tf_op jit(solution)/shard_map/ppermute | solution.py:594
  1477.4 11.3 sort.15
  1489.7 54.5 %collective-permute-done.28.rest_4_ = f32[1536,512]{1,0:T(8,128)} collective-permute-done((f32[1536,512]{1,0:T(8,128)}, f32[1536,512]{1,0:T(8,128)}, u32[]{:S(2)}, u32[]{:S(2)}) %collective-permute-start.28) | collective-permute-done | bytes 3145760 | tf_op jit(solution)/shard_map/ppermute | solution.py:594
  1544.2 1.6 collective-permute-start.32
  1545.8 43.4 %collective-permute-done.24 = f32[512,1024]{1,0:T(8,128)} collective-permute-done((f32[512,1024]{1,0:T(8,128)S(1)}, f32[512,1024]{1,0:T(8,128)}, u32[]{:S(2)}, u32[]{:S(2)}) %collective-permute-start.24) | collective-permute-done | bytes 2097184 | tf_op jit(solution)/shard_map/ppermute | solution.py:594
  1590.7 4.2 pad_maximum_fusion
  1597.8 3.3 add.99
  1601.1 7.9 constant_dynamic-update-slice_fusion.21
  1609.0 7.9 constant_dynamic-update-slice_fusion.20
  1616.9 7.9 constant_dynamic-update-slice_fusion.19
  1624.9 107.6 %row_sums.1 = f32[25152,512]{1,0:T(8,128)} custom-call(s32[18432]{0:T(1024)} %get-tuple-element.85.order_ref, s32[18432]{0:T(1024)} %get-tuple-element.86.id_ref, s32[13]{0:T(128)} %convert_reduce_fusion.b_ref, f32[1536,512]{1,0:T(8,128)} %get-tuple-element.87.rest_0_, f32[1536,512]{1,0:T(8,128)} %get-tuple-element.88.rest_1_, ...), custom_call_target="tpu_custom_call" | custom-call | flops 150000000 | bytes 89260032 | tf_op jit(solution)/shard_map/row_sums/pallas_call | solution.py:567
  (208 shorter events, 53.1 us)
Async XLA Ops:
  1.3 5.9 collective-permute-start
  3.7 4.6 copy-start.14
  3.7 4.5 copy-start.20
  8.0 26.7 %copy-start.6 = (s32[24,192]{1,0:T(8,128)}, s32[24,192]{1,0:T(8,128)S(1)}, u32[]{:S(2)}) copy-start(s32[24,192]{1,0:T(8,128)S(1)} %get-tuple-element.112) | copy-start | bytes 55300
  25.6 3.8 copy-start.18
  25.6 3.9 copy-start.19
  28.1 6.6 copy-start
  28.1 70.2 %collective-permute-start.1 = (f32[1536,512]{1,0:T(8,128)S(1)}, f32[1536,512]{1,0:T(8,128)}, u32[]{:S(2)}, u32[]{:S(2)}) collective-permute-start(f32[1536,512]{1,0:T(8,128)S(1)} %convert_select_fusion.2.own_ref), channel_id=1, source_target_pairs={{0,4},{4,0},{1,5},{5,1},{2,6},{6,2},{3,7},{7,3}} | collective-permute-start | bytes 9437192 | tf_op jit(solution)/shard_map/ppermute | solution.py:597
  29.4 5.3 copy-start.8
  30.1 5.1 copy-start.9
  70.8 4.2 copy-start.1
  74.5 166.5 %collective-permute-start.10 = (f32[1536,512]{1,0:T(8,128)}, f32[1536,512]{1,0:T(8,128)}, u32[]{:S(2)}, u32[]{:S(2)}) collective-permute-start(f32[1536,512]{1,0:T(8,128)} %convert_select_fusion.own_ref), channel_id=1, source_target_pairs={{0,4},{4,0},{1,5},{5,1},{2,6},{6,2},{3,7},{7,3}} | collective-permute-start | bytes 9437192 | tf_op jit(solution)/shard_map/ppermute | solution.py:597
  77.6 154.0 %collective-permute-start.6 = (f32[1536,512]{1,0:T(8,128)}, f32[1536,512]{1,0:T(8,128)}, u32[]{:S(2)}, u32[]{:S(2)}) collective-permute-start(f32[1536,512]{1,0:T(8,128)} %convert_select_fusion.1.own_ref), channel_id=1, source_target_pairs={{0,4},{4,0},{1,5},{5,1},{2,6},{6,2},{3,7},{7,3}} | collective-permute-start | bytes 9437192 | tf_op jit(solution)/shard_map/ppermute | solution.py:597
  106.2 142.8 %collective-permute-start.2 = (f32[1536,512]{1,0:T(8,128)}, f32[1536,512]{1,0:T(8,128)}, u32[]{:S(2)}, u32[]{:S(2)}) collective-permute-start(f32[1536,512]{1,0:T(8,128)} %front.3.refs_0_), channel_id=1, source_target_pairs={{0,1},{1,0},{2,3},{3,2},{4,5},{5,4},{6,7},{7,6}} | collective-permute-start | bytes 9437192 | tf_op jit(solution)/shard_map/ppermute | solution.py:591
  107.5 3.6 collective-permute-start.25
  108.5 3.8 collective-permute-start.3
  111.1 5.7 collective-permute-start.26
  239.1 217.9 %collective-permute-start.38 = (f32[1536,512]{1,0:T(8,128)}, f32[1536,512]{1,0:T(8,128)}, u32[]{:S(2)}, u32[]{:S(2)}) collective-permute-start(f32[1536,512]{1,0:T(8,128)} %front.4.refs_0_), channel_id=1, source_target_pairs={{0,2},{2,0},{1,3},{3,1},{4,6},{6,4},{5,7},{7,5}} | collective-permute-start | bytes 9437192 | tf_op jit(solution)/shard_map/ppermute | solution.py:594
  239.3 148.0 %collective-permute-start.7 = (f32[1536,512]{1,0:T(8,128)}, f32[1536,512]{1,0:T(8,128)}, u32[]{:S(2)}, u32[]{:S(2)}) collective-permute-start(f32[1536,512]{1,0:T(8,128)} %front.4.refs_0_), channel_id=1, source_target_pairs={{0,1},{1,0},{2,3},{3,2},{4,5},{5,4},{6,7},{7,6}} | collective-permute-start | bytes 9437192 | tf_op jit(solution)/shard_map/ppermute | solution.py:591
  248.6 211.0 %collective-permute-start.36 = (f32[1536,512]{1,0:T(8,128)}, f32[1536,512]{1,0:T(8,128)}, u32[]{:S(2)}, u32[]{:S(2)}) collective-permute-start(f32[1536,512]{1,0:T(8,128)} %front.5.refs_0_), channel_id=1, source_target_pairs={{0,2},{2,0},{1,3},{3,1},{4,6},{6,4},{5,7},{7,5}} | collective-permute-start | bytes 9437192 | tf_op jit(solution)/shard_map/ppermute | solution.py:594
  248.6 69.8 %collective-permute-start.11 = (f32[1536,512]{1,0:T(8,128)}, f32[1536,512]{1,0:T(8,128)}, u32[]{:S(2)}, u32[]{:S(2)}) collective-permute-start(f32[1536,512]{1,0:T(8,128)} %front.5.refs_0_), channel_id=1, source_target_pairs={{0,1},{1,0},{2,3},{3,2},{4,5},{5,4},{6,7},{7,6}} | collective-permute-start | bytes 9437192 | tf_op jit(solution)/shard_map/ppermute | solution.py:591
  249.0 211.0 %collective-permute-start.40 = (f32[1536,512]{1,0:T(8,128)}, f32[1536,512]{1,0:T(8,128)}, u32[]{:S(2)}, u32[]{:S(2)}) collective-permute-start(f32[1536,512]{1,0:T(8,128)} %front.3.refs_0_), channel_id=1, source_target_pairs={{0,2},{2,0},{1,3},{3,1},{4,6},{6,4},{5,7},{7,5}} | collective-permute-start | bytes 9437192 | tf_op jit(solution)/shard_map/ppermute | solution.py:594
  318.4 141.8 %collective-permute-start.4 = (f32[2,3072]{1,0:T(2,128)}, f32[2,3072]{1,0:T(2,128)}, u32[]{:S(2)}, u32[]{:S(2)}) collective-permute-start(f32[2,3072]{1,0:T(2,128)} %get-tuple-element.54.a_ref), channel_id=1, source_target_pairs={{0,1},{1,0},{2,3},{3,2},{4,5},{5,4},{6,7},{7,6}} | collective-permute-start | bytes 73736 | tf_op jit(solution)/shard_map/ppermute | solution.py:591
  387.3 67.9 %collective-permute-start.12 = (f32[2,3072]{1,0:T(2,128)}, f32[2,3072]{1,0:T(2,128)}, u32[]{:S(2)}, u32[]{:S(2)}) collective-permute-start(f32[2,3072]{1,0:T(2,128)} %get-tuple-element.60.a_ref), channel_id=1, source_target_pairs={{0,1},{1,0},{2,3},{3,2},{4,5},{5,4},{6,7},{7,6}} | collective-permute-start | bytes 73736 | tf_op jit(solution)/shard_map/ppermute | solution.py:591
  455.2 6.7 collective-permute-start.8
  457.1 6.9 collective-permute-start.13
  459.6 361.4 %collective-permute-start.39 = (f32[1536,512]{1,0:T(8,128)}, f32[1536,512]{1,0:T(8,128)}, u32[]{:S(2)}, u32[]{:S(2)}) collective-permute-start(f32[1536,512]{1,0:T(8,128)} %collective-permute-done.38.refs_2_), channel_id=1, source_target_pairs={{0,1},{1,0},{2,3},{3,2},{4,5},{5,4},{6,7},{7,6}} | collective-permute-start | bytes 9437192 | tf_op jit(solution)/shard_map/ppermute | solution.py:591
  460.0 361.6 %collective-permute-start.37 = (f32[1536,512]{1,0:T(8,128)}, f32[1536,512]{1,0:T(8,128)}, u32[]{:S(2)}, u32[]{:S(2)}) collective-permute-start(f32[1536,512]{1,0:T(8,128)} %collective-permute-done.36.refs_0_), channel_id=1, source_target_pairs={{0,1},{1,0},{2,3},{3,2},{4,5},{5,4},{6,7},{7,6}} | collective-permute-start | bytes 9437192 | tf_op jit(solution)/shard_map/ppermute | solution.py:591
  460.2 361.4 %collective-permute-start.41 = (f32[1536,512]{1,0:T(8,128)}, f32[1536,512]{1,0:T(8,128)}, u32[]{:S(2)}, u32[]{:S(2)}) collective-permute-start(f32[1536,512]{1,0:T(8,128)} %collective-permute-done.40.refs_4_), channel_id=1, source_target_pairs={{0,1},{1,0},{2,3},{3,2},{4,5},{5,4},{6,7},{7,6}} | collective-permute-start | bytes 9437192 | tf_op jit(solution)/shard_map/ppermute | solution.py:591
  461.9 112.9 %collective-permute-start.5 = (f32[2,3072]{1,0:T(2,128)}, f32[2,3072]{1,0:T(2,128)}, u32[]{:S(2)}, u32[]{:S(2)}) collective-permute-start(f32[2,3072]{1,0:T(2,128)} %merge_stats.6.a_ref), channel_id=1, source_target_pairs={{0,4},{4,0},{1,5},{5,1},{2,6},{6,2},{3,7},{7,3}} | collective-permute-start | bytes 73736 | tf_op jit(solution)/shard_map/ppermute | solution.py:597
  463.9 112.9 %collective-permute-start.9 = (f32[2,3072]{1,0:T(2,128)}, f32[2,3072]{1,0:T(2,128)}, u32[]{:S(2)}, u32[]{:S(2)}) collective-permute-start(f32[2,3072]{1,0:T(2,128)} %merge_stats.8.a_ref), channel_id=1, source_target_pairs={{0,4},{4,0},{1,5},{5,1},{2,6},{6,2},{3,7},{7,3}} | collective-permute-start | bytes 73736 | tf_op jit(solution)/shard_map/ppermute | solution.py:597
  574.9 238.7 %collective-permute-start.42 = (f32[1,3072]{1,0:T(1,128)}, f32[1,3072]{1,0:T(1,128)}, u32[]{:S(2)}, u32[]{:S(2)}) collective-permute-start(f32[1,3072]{1,0:T(1,128)} %get-tuple-element.61.le_ref), channel_id=1, source_target_pairs={{0,2},{2,0},{1,3},{3,1},{4,6},{6,4},{5,7},{7,5}} | collective-permute-start | bytes 36872 | tf_op jit(solution)/shard_map/ppermute | solution.py:594
  576.8 242.9 %collective-permute-start.44 = (f32[1,3072]{1,0:T(1,128)}, f32[1,3072]{1,0:T(1,128)}, u32[]{:S(2)}, u32[]{:S(2)}) collective-permute-start(f32[1,3072]{1,0:T(1,128)} %get-tuple-element.55.le_ref), channel_id=1, source_target_pairs={{0,2},{2,0},{1,3},{3,1},{4,6},{6,4},{5,7},{7,5}} | collective-permute-start | bytes 36872 | tf_op jit(solution)/shard_map/ppermute | solution.py:594
  813.6 2.8 collective-permute-start.43
  816.4 130.0 %collective-permute-start.18 = (f32[512,1536]{1,0:T(8,128)}, f32[512,1536]{1,0:T(8,128)}, u32[]{:S(2)}, u32[]{:S(2)}) collective-permute-start(f32[512,1536]{1,0:T(8,128)} %get-tuple-element.69), channel_id=1, source_target_pairs={{0,1},{1,0},{2,3},{3,2},{4,5},{5,4},{6,7},{7,6}} | collective-permute-start | bytes 9437192 | tf_op jit(solution)/shard_map/ppermute | solution.py:591
  819.7 132.3 %collective-permute-start.14 = (f32[512,1536]{1,0:T(8,128)}, f32[512,1536]{1,0:T(8,128)}, u32[]{:S(2)}, u32[]{:S(2)}) collective-permute-start(f32[512,1536]{1,0:T(8,128)} %get-tuple-element.65), channel_id=1, source_target_pairs={{0,1},{1,0},{2,3},{3,2},{4,5},{5,4},{6,7},{7,6}} | collective-permute-start | bytes 9437192 | tf_op jit(solution)/shard_map/ppermute | solution.py:591
  821.0 136.5 %collective-permute-start.16 = (f32[512,1536]{1,0:T(8,128)}, f32[512,1536]{1,0:T(8,128)}, u32[]{:S(2)}, u32[]{:S(2)}) collective-permute-start(f32[512,1536]{1,0:T(8,128)} %get-tuple-element.67), channel_id=1, source_target_pairs={{0,1},{1,0},{2,3},{3,2},{4,5},{5,4},{6,7},{7,6}} | collective-permute-start | bytes 9437192 | tf_op jit(solution)/shard_map/ppermute | solution.py:591
  946.4 5.7 copy-start.5
  951.7 120.3 %collective-permute-start.19 = (f32[512,1536]{1,0:T(8,128)}, f32[512,1536]{1,0:T(8,128)}, u32[]{:S(2)}, u32[]{:S(2)}) collective-permute-start(f32[512,1536]{1,0:T(8,128)} %add.92.a_ref), channel_id=1, source_target_pairs={{0,4},{4,0},{1,5},{5,1},{2,6},{6,2},{3,7},{7,3}} | collective-permute-start | bytes 9437192 | tf_op jit(solution)/shard_map/ppermute | solution.py:597
  952.0 5.5 copy-start.4
  956.4 214.8 %collective-permute-start.15 = (f32[512,1536]{1,0:T(8,128)}, f32[512,1536]{1,0:T(8,128)}, u32[]{:S(2)}, u32[]{:S(2)}) collective-permute-start(f32[512,1536]{1,0:T(8,128)} %add.90.a_ref), channel_id=1, source_target_pairs={{0,4},{4,0},{1,5},{5,1},{2,6},{6,2},{3,7},{7,3}} | collective-permute-start | bytes 9437192 | tf_op jit(solution)/shard_map/ppermute | solution.py:597
  961.6 194.8 %collective-permute-start.17 = (f32[512,1536]{1,0:T(8,128)}, f32[512,1536]{1,0:T(8,128)}, u32[]{:S(2)}, u32[]{:S(2)}) collective-permute-start(f32[512,1536]{1,0:T(8,128)} %add.91.a_ref), channel_id=1, source_target_pairs={{0,4},{4,0},{1,5},{5,1},{2,6},{6,2},{3,7},{7,3}} | collective-permute-start | bytes 9437192 | tf_op jit(solution)/shard_map/ppermute | solution.py:597
  1187.7 111.3 %collective-permute-start.20 = (f32[8,512]{1,0:T(8,128)}, f32[8,512]{1,0:T(8,128)}, u32[]{:S(2)}, u32[]{:S(2)}) collective-permute-start(f32[8,512]{1,0:T(8,128)} %concatenate.47), channel_id=1, source_target_pairs={{0,1},{1,0},{2,3},{3,2},{4,5},{5,4},{6,7},{7,6}} | collective-permute-start | bytes 49160 | tf_op jit(solution)/shard_map/ppermute | solution.py:591
  1298.4 291.8 %collective-permute-start.47 = (f32[4192,512]{1,0:T(8,128)}, f32[4192,512]{1,0:T(8,128)}, u32[]{:S(2)}, u32[]{:S(2)}) collective-permute-start(f32[4192,512]{1,0:T(8,128)} %get-tuple-element.96), channel_id=1, source_target_pairs={{0,1},{1,0},{2,3},{3,2},{4,5},{5,4},{6,7},{7,6}} | collective-permute-start | bytes 25755656 | tf_op jit(solution)/shard_map/ppermute | solution.py:591
  1298.5 291.7 %collective-permute-start.46 = (f32[4192,512]{1,0:T(8,128)}, f32[4192,512]{1,0:T(8,128)}, u32[]{:S(2)}, u32[]{:S(2)}) collective-permute-start(f32[4192,512]{1,0:T(8,128)} %get-tuple-element.95), channel_id=1, source_target_pairs={{0,1},{1,0},{2,3},{3,2},{4,5},{5,4},{6,7},{7,6}} | collective-permute-start | bytes 25755656 | tf_op jit(solution)/shard_map/ppermute | solution.py:591
  1298.9 291.8 %collective-permute-start.45 = (f32[4192,512]{1,0:T(8,128)}, f32[4192,512]{1,0:T(8,128)}, u32[]{:S(2)}, u32[]{:S(2)}) collective-permute-start(f32[4192,512]{1,0:T(8,128)} %get-tuple-element.94), channel_id=1, source_target_pairs={{0,1},{1,0},{2,3},{3,2},{4,5},{5,4},{6,7},{7,6}} | collective-permute-start | bytes 25755656 | tf_op jit(solution)/shard_map/ppermute | solution.py:591
  1299.7 2.6 collective-permute-start.21
  1302.3 2.5 collective-permute-start.22
  1302.6 36.9 %collective-permute-start.23 = (f32[512,1024]{1,0:T(8,128)}, f32[512,1024]{1,0:T(8,128)S(1)}, u32[]{:S(2)}, u32[]{:S(2)}) collective-permute-start(f32[512,1024]{1,0:T(8,128)} %get-tuple-element.84), channel_id=1, source_target_pairs={{0,1},{1,0},{2,3},{3,2},{4,5},{5,4},{6,7},{7,6}} | collective-permute-start | bytes 6291464 | tf_op jit(solution)/shard_map/ppermute | solution.py:591
  1304.8 39.3 %collective-permute-start.30 = (f32[1536,512]{1,0:T(8,128)}, f32[1536,512]{1,0:T(8,128)S(1)}, u32[]{:S(2)}, u32[]{:S(2)}) collective-permute-start(f32[1536,512]{1,0:T(8,128)} %get-tuple-element.87.rest_0_), channel_id=1, source_target_pairs={{0,1},{1,0},{2,3},{3,2},{4,5},{5,4},{6,7},{7,6}} | collective-permute-start | bytes 9437192 | tf_op jit(solution)/shard_map/ppermute | solution.py:591
  1339.6 69.7 %collective-permute-start.27 = (f32[1536,512]{1,0:T(8,128)}, f32[1536,512]{1,0:T(8,128)S(1)}, u32[]{:S(2)}, u32[]{:S(2)}) collective-permute-start(f32[1536,512]{1,0:T(8,128)} %get-tuple-element.87.rest_0_), channel_id=1, source_target_pairs={{0,2},{2,0},{1,3},{3,1},{4,6},{6,4},{5,7},{7,5}} | collective-permute-start | bytes 9437192 | tf_op jit(solution)/shard_map/ppermute | solution.py:594
  1344.1 65.2 %copy-start.2 = (f32[1536,512]{1,0:T(8,128)}, f32[1536,512]{1,0:T(8,128)S(1)}, u32[]{:S(2)}) copy-start(f32[1536,512]{1,0:T(8,128)S(1)} %collective-permute-done.30.rest_6_) | copy-start | bytes 9437188
  1344.1 132.7 %collective-permute-start.29 = (f32[1536,512]{1,0:T(8,128)}, f32[1536,512]{1,0:T(8,128)}, u32[]{:S(2)}, u32[]{:S(2)}) collective-permute-start(f32[1536,512]{1,0:T(8,128)} %get-tuple-element.89.rest_2_), channel_id=1, source_target_pairs={{0,2},{2,0},{1,3},{3,1},{4,6},{6,4},{5,7},{7,5}} | collective-permute-start | bytes 9437192 | tf_op jit(solution)/shard_map/ppermute | solution.py:594
  1411.0 66.2 %copy-start.7 = (s32[24,192]{1,0:T(8,128)S(1)}, s32[24,192]{1,0:T(8,128)}, u32[]{:S(2)}) copy-start(s32[24,192]{1,0:T(8,128)} %copy-done.6) | copy-start | bytes 55300
  1411.0 66.3 %copy-start.11 = (s32[1,3,1536]{2,1,0:T(4,128)S(1)}, s32[1,3,1536]{2,1,0:T(4,128)}, u32[]{:S(2)}) copy-start(s32[1,3,1536]{2,1,0:T(4,128)} %get-tuple-element.119) | copy-start | bytes 55300
  1411.0 66.3 %copy-start.10 = (s32[1,3,1536]{2,1,0:T(4,128)S(1)}, s32[1,3,1536]{2,1,0:T(4,128)}, u32[]{:S(2)}) copy-start(s32[1,3,1536]{2,1,0:T(4,128)} %get-tuple-element.120) | copy-start | bytes 55300
  1411.0 66.3 %copy-start.12 = (s32[1,3,1536]{2,1,0:T(4,128)S(1)}, s32[1,3,1536]{2,1,0:T(4,128)}, u32[]{:S(2)}) copy-start(s32[1,3,1536]{2,1,0:T(4,128)} %get-tuple-element.117) | copy-start | bytes 55300
  1411.0 133.2 %collective-permute-start.28 = (f32[1536,512]{1,0:T(8,128)}, f32[1536,512]{1,0:T(8,128)}, u32[]{:S(2)}, u32[]{:S(2)}) collective-permute-start(f32[1536,512]{1,0:T(8,128)} %get-tuple-element.88.rest_1_), channel_id=1, source_target_pairs={{0,2},{2,0},{1,3},{3,1},{4,6},{6,4},{5,7},{7,5}} | collective-permute-start | bytes 9437192 | tf_op jit(solution)/shard_map/ppermute | solution.py:594
  1476.8 112.4 %collective-permute-start.24 = (f32[512,1024]{1,0:T(8,128)S(1)}, f32[512,1024]{1,0:T(8,128)}, u32[]{:S(2)}, u32[]{:S(2)}) collective-permute-start(f32[512,1024]{1,0:T(8,128)S(1)} %add.98), channel_id=1, source_target_pairs={{0,2},{2,0},{1,3},{3,1},{4,6},{6,4},{5,7},{7,5}} | collective-permute-start | bytes 6291464 | tf_op jit(solution)/shard_map/ppermute | solution.py:594
  1544.2 80.6 %collective-permute-start.32 = (f32[1536,512]{1,0:T(8,128)}, f32[1536,512]{1,0:T(8,128)}, u32[]{:S(2)}, u32[]{:S(2)}) collective-permute-start(f32[1536,512]{1,0:T(8,128)} %get-tuple-element.89.rest_2_), channel_id=1, source_target_pairs={{0,1},{1,0},{2,3},{3,2},{4,5},{5,4},{6,7},{7,6}} | collective-permute-start | bytes 9437192 | tf_op jit(solution)/shard_map/ppermute | solution.py:591
  1589.2 35.7 %collective-permute-start.31 = (f32[1536,512]{1,0:T(8,128)}, f32[1536,512]{1,0:T(8,128)}, u32[]{:S(2)}, u32[]{:S(2)}) collective-permute-start(f32[1536,512]{1,0:T(8,128)} %get-tuple-element.88.rest_1_), channel_id=1, source_target_pairs={{0,1},{1,0},{2,3},{3,2},{4,5},{5,4},{6,7},{7,6}} | collective-permute-start | bytes 9437192 | tf_op jit(solution)/shard_map/ppermute | solution.py:591
  1590.2 34.7 %collective-permute-start.33 = (f32[1536,512]{1,0:T(8,128)}, f32[1536,512]{1,0:T(8,128)}, u32[]{:S(2)}, u32[]{:S(2)}) collective-permute-start(f32[1536,512]{1,0:T(8,128)} %copy-done.3), channel_id=1, source_target_pairs={{0,1},{1,0},{2,3},{3,2},{4,5},{5,4},{6,7},{7,6}} | collective-permute-start | bytes 9437192 | tf_op jit(solution)/shard_map/ppermute | solution.py:591
  1590.2 34.7 %collective-permute-start.35 = (f32[1536,512]{1,0:T(8,128)}, f32[1536,512]{1,0:T(8,128)}, u32[]{:S(2)}, u32[]{:S(2)}) collective-permute-start(f32[1536,512]{1,0:T(8,128)} %collective-permute-done.29.rest_5_), channel_id=1, source_target_pairs={{0,1},{1,0},{2,3},{3,2},{4,5},{5,4},{6,7},{7,6}} | collective-permute-start | bytes 9437192 | tf_op jit(solution)/shard_map/ppermute | solution.py:591
  1590.7 34.2 %collective-permute-start.34 = (f32[1536,512]{1,0:T(8,128)}, f32[1536,512]{1,0:T(8,128)}, u32[]{:S(2)}, u32[]{:S(2)}) collective-permute-start(f32[1536,512]{1,0:T(8,128)} %collective-permute-done.28.rest_4_), channel_id=1, source_target_pairs={{0,1},{1,0},{2,3},{3,2},{4,5},{5,4},{6,7},{7,6}} | collective-permute-start | bytes 9437192 | tf_op jit(solution)/shard_map/ppermute | solution.py:591
  (5 other events, 7.6 us)

commit v2 on v1

v2 whole, which is shorter than its diff:
```python
import functools

import jax
import jax.numpy as jnp
from jax import lax
from jax.experimental import pallas as pl
from jax.experimental.pallas import tpu as pltpu
from jax.sharding import PartitionSpec as P


MTP_WEIGHT = 0.3
NORM_EPS = 1e-6
LOG2E = 1.4426950408889634
LN2 = 0.6931471805599453
NEG = -1e30
V_TILE = 2096
N_CHUNK = 3
VMEM_BYTES = 67043328
f32, bf16 = jnp.float32, jnp.bfloat16
ALL, ORIGIN, WIDTH, STEP, LANES, PACK, SUB, TWO = Ellipsis, (0, 0), 512, 768, 256, 16, 8, 2
NT = (((1,), (1,)), ((), ()))
NN = (((1,), (0,)), ((), ()))
TN = (((0,), (0,)), ((), ()))
CORE_SWAP = [(0, 1), (1, 0), (2, 3), (3, 2)]
X_SWAP = [(0, 2), (2, 0), (1, 3), (3, 1)]
Y_SWAP = [(0, 1), (1, 0)]


def cuts(size, pieces, step):
    edges = [((size * i) // pieces) // step * step for i in range(pieces)] + [size]
    return list(zip(edges[:-1], edges[1:]))


def tree(op, items):
    items = list(items)
    while len(items) > 1:
        items = [op(items[i], items[i + 1]) if i + 1 < len(items) else items[i] for i in range(0, len(items), 2)]
    return items[0]


def alternate(first, second):
    out = []
    for i in range(max(len(first), len(second))):
        out += first[i:i + 1] + second[i:i + 1]
    return out


def interleave(dots, passes):
    done = 0
    for i, dot in enumerate(dots):
        dot()
        while done < len(passes) and (done + 1) * len(dots) <= (i + 1) * len(passes):
            passes[done]()
            done += 1
    for piece in passes[done:]:
        piece()


def grad_piece(y_ref, g_ref, lab_ref, le_ref, wt_ref, hit_ref, base, row0, lanes, scale, l, r0, r1):
    sl = pl.ds(pl.multiple_of(base + l, lanes), lanes)
    lab = lab_ref[:, sl] - (lax.broadcasted_iota(jnp.int32, (SUB, lanes), 0) + row0)
    le = jnp.broadcast_to(le_ref[:, sl], (SUB, lanes))
    wt = jnp.broadcast_to(wt_ref[:, sl], (SUB, lanes))
    if hit_ref is not None:
        acc = [hit_ref[:SUB, sl], hit_ref[SUB:, sl]]
    for r in range(r0, r1, PACK):
        halves = []
        for q in (0, SUB):
            y = y_ref[r + q:r + q + SUB, l:l + lanes]
            if scale:
                y = y * LOG2E
            hit = lab == (r + q)
            e = jnp.exp2(y - le)
            halves.append(jnp.where(hit, e - wt, e))
            if hit_ref is not None:
                acc[q // SUB] = jnp.where(hit, y, acc[q // SUB])
        g_ref[r:r + PACK, l:l + lanes] = jnp.concatenate(halves, axis=0).astype(bf16)
    if hit_ref is not None:
        hit_ref[:SUB, sl] = acc[0]
        hit_ref[SUB:, sl] = acc[1]


def once():
    return {}


def params():
    return pltpu.CompilerParams(vmem_limit_bytes=VMEM_BYTES)


def cost(dots, rows, n, extra):
    return pl.CostEstimate(flops=TWO * dots * rows * n * WIDTH, bytes_accessed=extra, transcendentals=rows * n)


def rms_parts(x):
    return lax.rsqrt(jnp.mean(x * x, axis=-1, keepdims=True) + NORM_EPS)


def rms_back(dy, x, r, gain):
    dg = dy * gain
    dx = r * dg - x * (r * r * r) * jnp.mean(dg * x, axis=-1, keepdims=True)
    n, width = x.shape
    return dx, jnp.sum((dy * x * r).reshape(n // SUB, SUB, width), axis=0)


def mix(h_ref, own_ref, recv_ref, w_ref, g_ref):
    h = h_ref[ALL].astype(f32)
    e = own_ref[ALL] + recv_ref[ALL]
    rh, re = rms_parts(h), rms_parts(e)
    joined = jnp.concatenate([(h * rh * g_ref[0:1, :]).astype(bf16), (e * re * g_ref[1:2, :]).astype(bf16)], axis=1)
    mixed = lax.dot_general(joined, w_ref[ALL], NT, preferred_element_type=f32)
    return h, e, rh, re, joined, mixed, rms_parts(mixed)


def tiles_of(tile, *widths):
    return [pl.BlockSpec((tile, w), lambda i: (i, 0)) for w in widths]


def front_kernel(hid, own, recv, w_proj, gains):
    n, width = hid.shape
    tile = WIDTH

    def body(h_ref, own_ref, recv_ref, w_ref, g_ref, out_ref):
        mixed, rf = mix(h_ref, own_ref, recv_ref, w_ref, g_ref)[5:]
        out_ref[ALL] = mixed * rf * g_ref[2:3, :]

    return pl.pallas_call(
        body,
        grid=(n // tile,),
        in_specs=tiles_of(tile, width, width, width) + [
            pl.BlockSpec((width, TWO * width), lambda i: ORIGIN), pl.BlockSpec((3, width), lambda i: ORIGIN)],
        out_specs=tiles_of(tile, width)[0],
        out_shape=jax.ShapeDtypeStruct((n, width), f32),
        compiler_params=params(),
        cost_estimate=pl.CostEstimate(flops=4 * n * width * width, bytes_accessed=14 * n * width, transcendentals=3 * n),
        name="front",
    )(hid, own, recv, w_proj, gains)


def back_kernel(hid, own, recv, w_proj, gains, df_mine, df_recv, chunk, totals):
    n, width = hid.shape
    tile = WIDTH

    def body(h_ref, own_ref, recv_ref, w_ref, g_ref, a_ref, b_ref, *rest):
        dh_ref, de_ref, dw_ref, dg_ref = rest[-4:]
        h, e, rh, re, joined, mixed, rf = mix(h_ref, own_ref, recv_ref, w_ref, g_ref)
        df = (a_ref[ALL] + b_ref[ALL]).T
        du, dgf = rms_back(df, mixed, rf, g_ref[2:3, :])
        du = du.astype(bf16)
        dx = lax.dot_general(du, w_ref[ALL], NN, preferred_element_type=f32)
        dh, dgh = rms_back(dx[:, :width], h, rh, g_ref[0:1, :])
        de, dge = rms_back(dx[:, width:], e, re, g_ref[1:2, :])
        dh_ref[ALL] = dh.astype(bf16)
        de_ref[ALL] = de
        dw = lax.dot_general(du, joined, TN, preferred_element_type=f32)

        @pl.when(pl.program_id(0) == 0)
        def _():
            dw_ref[ALL] = rest[0][ALL] if totals else jnp.zeros_like(dw_ref)
            dg_ref[ALL] = rest[1][ALL] if totals else jnp.zeros_like(dg_ref)

        dw_ref[ALL] += dw
        dg_ref[0:SUB, :] += dgh
        dg_ref[SUB:PACK, :] += dge
        dg_ref[PACK:24, :] += dgf

    cols = pl.BlockSpec((width, tile), lambda i: (0, i))
    sums = [pl.BlockSpec((width, TWO * width), lambda i: ORIGIN), pl.BlockSpec((24, width), lambda i: ORIGIN)]
    return pl.pallas_call(
        body,
        grid=(n // tile,),
        in_specs=tiles_of(tile, width, width, width) + [
            pl.BlockSpec((width, TWO * width), lambda i: ORIGIN), pl.BlockSpec((3, width), lambda i: ORIGIN), cols, cols]
        + (sums + [pl.BlockSpec(memory_space=pl.ANY)])[:len(totals)],
        input_output_aliases={9: 0} if totals else {},
        out_specs=[pl.BlockSpec((tile, width), lambda i: (chunk * (n // tile) + i, 0))] + tiles_of(tile, width) + sums,
        out_shape=[
            jax.ShapeDtypeStruct((N_CHUNK * n, width), bf16), jax.ShapeDtypeStruct((n, width), f32),
            jax.ShapeDtypeStruct((width, TWO * width), f32), jax.ShapeDtypeStruct((24, width), f32)],
        compiler_params=params(),
        cost_estimate=pl.CostEstimate(flops=12 * n * width * width, bytes_accessed=24 * n * width, transcendentals=3 * n),
        name="back",
    )(hid, own, recv, w_proj, gains, df_mine, df_recv, *totals)


def merge_halves(mine, mate):
    n = mine.shape[1]

    def body(a_ref, b_ref, out_ref):
        b = jnp.concatenate([b_ref[:, n // TWO:], b_ref[:, :n // TWO]], axis=1)
        out_ref[ALL] = merged(a_ref[ALL], b)

    return pl.pallas_call(body, out_shape=jax.ShapeDtypeStruct((2, n), f32), name="merge_halves")(mine, mate)


def merged(a, b):
    top = jnp.maximum(a[0:1, :], b[0:1, :])
    total = a[1:2, :] * jnp.exp2(a[0:1, :] - top) + b[1:2, :] * jnp.exp2(b[0:1, :] - top)
    return jnp.concatenate([top, total], axis=0)


def finish_stats(mine, other, wt, chunk, into):
    n = mine.shape[1]

    def body(a_ref, b_ref, wt_ref, *rest):
        both = merged(a_ref[ALL], b_ref[ALL])
        lse = both[0:1, :] + jnp.log2(both[1:2, :])
        rest[-2][ALL] = lse
        rest[-1][ALL] = lse - jnp.log2(wt_ref[ALL])

    here = pl.BlockSpec((1, n), lambda i: (0, chunk))
    block = pl.BlockSpec((2, n), lambda i: ORIGIN)
    return pl.pallas_call(
        body,
        grid=(1,),
        in_specs=[block, block, here] + [pl.BlockSpec(memory_space=pl.ANY)] * len(into),
        out_specs=[here, here],
        out_shape=[jax.ShapeDtypeStruct((1, N_CHUNK * n), f32)] * TWO,
        input_output_aliases={3: 0, 4: 1} if into else {},
        name="finish_stats",
    )(mine, other, wt, *into)


def round_rows(parts, total=None, slot=0, into=None):
    m, (n, width) = len(parts), parts[0].shape
    tile = STEP
    steps = n // tile
    total = m * n if total is None else total
    first = slot * m * steps

    def body(*refs):
        k = pl.program_id(0)
        for i in range(m):
            @pl.when(k == i)
            def _(i=i):
                refs[-1][ALL] = refs[i][ALL].astype(bf16)

    def spec(i):
        return pl.BlockSpec((tile, width), lambda k, b: (jnp.where(k == i, b, jnp.where(k > i, steps - 1, 0)), 0))

    extra = [] if into is None else [into]
    return pl.pallas_call(
        body,
        grid=(m, steps),
        in_specs=[spec(i) for i in range(m)] + [pl.BlockSpec(memory_space=pl.ANY)] * len(extra),
        out_specs=pl.BlockSpec((tile, width), lambda k, b: (first + k * steps + b, 0)),
        out_shape=jax.ShapeDtypeStruct((total, width), bf16),
        input_output_aliases={m: 0} if extra else {},
        compiler_params=params(),
        name="round_rows",
    )(*parts, *extra)


def logits_kernel(meta, out_tab, feats, rows, chunk, into):
    n = feats.shape[0] // N_CHUNK
    t, lanes, groups = STEP, LANES, 2
    nv, nj = rows // V_TILE, n // (TWO * t)
    extra = [] if into is None else [into]

    def stats(y_ref, m_ref, s_ref, start):
        for l in range(0, t, lanes):
            sl = pl.ds(pl.multiple_of(start + l, lanes), lanes)
            old = m_ref[:, sl]
            acc = [old] + [None] * (groups - 1)
            for i, r in enumerate(range(0, V_TILE, SUB)):
                x = y_ref[r:r + SUB, l:l + lanes]
                acc[i % groups] = x if acc[i % groups] is None else jnp.maximum(acc[i % groups], x)
            new = tree(jnp.maximum, acc)
            acc = [s_ref[:, sl] * jnp.exp2(old - new)] + [None] * (groups - 1)
            for i, r in enumerate(range(0, V_TILE, SUB)):
                x = jnp.exp2(y_ref[r:r + SUB, l:l + lanes] - new)
                acc[i % groups] = x if acc[i % groups] is None else acc[i % groups] + x
            s_ref[:, sl] = tree(jnp.add, acc)
            m_ref[:, sl] = new

    def body(meta_ref, w_ref, f_ref, *rest):
        y_ref, st_ref, ya, yb, m_ref, s_ref = rest[-6:]
        v, j = pl.program_id(0), pl.program_id(1)
        step = v * nj + j

        @pl.when(step == 0)
        def _():
            m_ref[ALL] = jnp.full_like(m_ref, NEG)
            s_ref[ALL] = jnp.zeros_like(s_ref)
            yb[ALL] = jnp.full_like(yb, TWO * NEG)

        base = pl.multiple_of(j * TWO * t, TWO * t)
        prev = pl.multiple_of(lax.rem(j + nj - 1, nj) * TWO * t, TWO * t)
        w = w_ref[ALL]

        def dot(start, buf, lo):
            y = lax.dot_general(w, f_ref[pl.ds(start, t), :], NT, preferred_element_type=f32) * LOG2E
            buf[ALL] = y
            y_ref[:, lo:lo + t] = y

        dot(base, ya, 0)
        stats(yb, m_ref, s_ref, prev + t)
        dot(base + t, yb, t)
        stats(ya, m_ref, s_ref, base)

        @pl.when(step == nv * nj - 1)
        def _():
            stats(yb, m_ref, s_ref, base + t)
            m = m_ref[ALL]
            top = jnp.max(m, axis=0, keepdims=True)
            st_ref[0:1, :] = top
            st_ref[1:2, :] = jnp.sum(s_ref[ALL] * jnp.exp2(m - top), axis=0, keepdims=True)

    grid_spec = pltpu.PrefetchScalarGridSpec(
        num_scalar_prefetch=1,
        grid=(nv, nj),
        in_specs=[
            pl.BlockSpec((V_TILE, WIDTH), lambda v, j, c: (c[0] * nv + v, 0)),
            pl.BlockSpec((n, WIDTH), lambda v, j, c: (chunk, 0), **once()),
        ] + [pl.BlockSpec(memory_space=pl.ANY)] * len(extra),
        out_specs=[pl.BlockSpec((V_TILE, TWO * t), lambda v, j, c: (v, chunk * nj + j)), pl.BlockSpec((2, n), lambda v, j, c: ORIGIN)],
        scratch_shapes=[pltpu.VMEM((V_TILE, t), f32)] * TWO + [pltpu.VMEM((SUB, n), f32)] * TWO,
    )
    return pl.pallas_call(
        body,
        grid_spec=grid_spec,
        out_shape=[jax.ShapeDtypeStruct((rows, N_CHUNK * n), f32), jax.ShapeDtypeStruct((2, n), f32)],
        input_output_aliases={3: 0} if extra else {},
        compiler_params=params(),
        cost_estimate=cost(1, rows, n, 4 * rows * n),
        name="logits",
    )(meta, out_tab, feats, *extra)


def own_kernel(meta, logits, feats, out_tab, lab, le, wt, kept, chunk, d_feats, d_out):
    rows, n_all = logits.shape
    whole = chunk is None
    n = n_all if whole else n_all // N_CHUNK
    half_n = n_all // N_CHUNK // TWO
    t, lanes, pm, pn, pr = STEP, LANES, 12, LANES, SUB
    nv = rows // V_TILE
    nk = nv // TWO
    n_tiles, nj = (1 if whole else nk + 1), n // t
    per_half = half_n // t
    last = n_tiles * nj
    at = 0 if whole else chunk

    def tile(m, k):
        keep = nk * m[1] + kept
        return keep if whole else jnp.where(k < nk, nk * (1 - m[1]) + k, keep)

    def body(meta_ref, y_ref, f_ref, w_ref, lab_ref, le_ref, wt_ref, *rest):
        rest = list(rest)
        df_in = rest.pop(0) if d_feats is not None else None
        dw_in = rest.pop(0) if d_out is not None else None
        if whole:
            dw_ref, df_ref, hit_ref, ga, gb = rest
        else:
            dw_ref, dfa_ref, dfb_ref, hit_ref, ga, gb, df_ref, sem = rest
        s = pl.program_id(0)
        k, j, pk, pj = s // nj, lax.rem(s, nj), (s - 1) // nj, lax.rem(s - 1 + nj, nj)
        base = pl.multiple_of(j * t, t)
        row0 = tile(meta_ref, k) * V_TILE
        pjc = lax.rem(pj, TWO * per_half)
        half = pjc // per_half
        half_start = (pjc - half * per_half) * t

        def fetch():
            return pltpu.make_async_copy(df_in.at[chunk], df_ref, sem)

        if whole:
            @pl.when((s > 0) & (pjc == 0))
            def _():
                df_ref[ALL] = jnp.zeros_like(df_ref) if df_in is None else df_in[ALL]

        @pl.when(s == 0)
        def _():
            if not whole:
                fetch().start()
            hit_ref[ALL] = jnp.zeros_like(hit_ref)
            dw_ref[ALL] = jnp.zeros_like(dw_ref) if dw_in is None else dw_in[ALL]

        def grads(g):
            return [
                functools.partial(grad_piece, y_ref, g, lab_ref, le_ref, wt_ref, hit_ref, base, row0, lanes, False, l, r0, r1)
                for l in range(0, t, lanes) for r0, r1 in cuts(V_TILE, pr, PACK)
            ]

        def dots(g, with_out):
            def out_piece(r0, r1):
                dw_ref[r0:r1, :] += lax.dot_general(g[r0:r1, :], f_ref[ALL], NN, preferred_element_type=f32)

            def feat_piece(l, k0, k1):
                sl = pl.ds(pl.multiple_of(half_start + l, pn), pn)
                df_ref[half, :, sl] += lax.dot_general(w_ref[k0:k1, :], g[k0:k1, l:l + pn], TN, preferred_element_type=f32)

            out = [functools.partial(out_piece, r0, r1) for r0, r1 in cuts(V_TILE, pm, PACK)] if with_out else []
            pk = [(0, V_TILE)] if with_out else [(0, WIDTH), (WIDTH, 1024), (1024, 1536), (1536, V_TILE)]
            return alternate(out, [functools.partial(feat_piece, l, k0, k1) for l in range(0, t, pn) for k0, k1 in pk])

        @pl.when(s == 0)
        def _():
            interleave([], grads(ga))

        if not whole:
            @pl.when(s == 1)
            def _():
                fetch().wait()

        for parity, (g_old, g_new) in enumerate([(gb, ga), (ga, gb)]):
            mid = (s > 0) & (s < last) & (lax.rem(s, 2) == parity)
            if whole:
                @pl.when(mid)
                def _():
                    interleave(dots(g_old, True), grads(g_new))
            else:
                @pl.when(mid & (pk == nk))
                def _():
                    interleave(dots(g_old, True), grads(g_new))

                @pl.when(mid & (pk < nk))
                def _():
                    interleave(dots(g_old, False), grads(g_new))

        @pl.when(s == last)
        def _():
            interleave(dots(ga if last % 2 == 1 else gb, True), [])
            if not whole:
                dfa_ref[ALL] = df_ref[0]
                dfb_ref[ALL] = df_ref[1]

    def now(s):
        return jnp.minimum(s, last - 1)

    def lag(s):
        return jnp.maximum(s - 1, 0) // nj

    def lag_j(s):
        return lax.rem(jnp.maximum(s - 1, 0), nj)

    by_chunk = pl.BlockSpec((None, 2, WIDTH, half_n), lambda s, c: (lag_j(s) // (TWO * per_half), 0, 0, 0))
    row = pl.BlockSpec((1, n), lambda s, c: (0, at), **once())
    out_blk = pl.BlockSpec((V_TILE, WIDTH), lambda s, c: ORIGIN, **once())
    in_specs = [
        pl.BlockSpec((V_TILE, t), lambda s, c: (tile(c, now(s) // nj), at * nj + lax.rem(now(s), nj))),
        pl.BlockSpec((t, WIDTH), lambda s, c: (at * nj + lag_j(s), 0)),
        pl.BlockSpec((V_TILE, WIDTH), lambda s, c: (c[0] * nv + tile(c, lag(s)), 0)),
        row, row, row,
    ]
    args = [logits, feats, out_tab, lab, le, wt]
    if d_feats is not None:
        in_specs.append(by_chunk if whole else pl.BlockSpec(memory_space=pl.ANY))
        args.append(d_feats)
    if d_out is not None:
        in_specs.append(out_blk)
        args.append(d_out)
    df_shape = (N_CHUNK, 2, WIDTH, half_n) if whole else (WIDTH, half_n)
    df_spec = by_chunk if whole else pl.BlockSpec(df_shape, lambda s, c: ORIGIN, **once())
    df_outs = 1 if whole else 2
    grid_spec = pltpu.PrefetchScalarGridSpec(
        num_scalar_prefetch=1,
        grid=(last + 1,),
        in_specs=in_specs,
        out_specs=[out_blk] + [df_spec] * df_outs + [pl.BlockSpec((PACK, n), lambda s, c: ORIGIN, **once())],
        scratch_shapes=[pltpu.VMEM((V_TILE, t), bf16)] * TWO
        + ([] if whole else [pltpu.VMEM((2, WIDTH, half_n), f32), pltpu.SemaphoreType.DMA(())]),
    )
    return pl.pallas_call(
        body,
        grid_spec=grid_spec,
        out_shape=[jax.ShapeDtypeStruct((V_TILE, WIDTH), f32)] + [jax.ShapeDtypeStruct(df_shape, f32)] * df_outs
        + [jax.ShapeDtypeStruct((PACK, n), f32)],
        compiler_params=params(),
        cost_estimate=cost(2, n_tiles * V_TILE, n, 4 * n_tiles * V_TILE * n),
        name="own",
    )(meta, *args)


def other_kernel(meta, feats, out_tab, lab, le, wt, acc, whole, kept):
    n = feats.shape[0]
    block = out_tab.shape[0]
    nv = block // TWO // V_TILE
    t, lanes, pz, pm, pr = STEP, LANES, 6, 6, 4
    last = n // t

    def tile(m):
        return (nv // TWO) * m[1] + kept

    def body(meta_ref, f_ref, fl_ref, w_ref, lab_ref, le_ref, wt_ref, in_ref, *rest):
        dw_ref, whole_ref, ya, yb, ga, gb = rest[-6:]
        s = pl.program_id(0)

        def start(k):
            return pl.multiple_of(jnp.clip(s - k, 0, last - 1) * t, t)

        row0 = tile(meta_ref) * V_TILE

        def logit_pieces(y):
            def piece(r0, r1):
                y[r0:r1, :] = lax.dot_general(w_ref[r0:r1, :], f_ref[ALL], NT, preferred_element_type=f32)

            return [functools.partial(piece, r0, r1) for r0, r1 in cuts(V_TILE, pz, PACK)]

        def out_pieces(g):
            def piece(r0, r1):
                dw_ref[r0:r1, :] += lax.dot_general(g[r0:r1, :], fl_ref[ALL], NN, preferred_element_type=f32)

            return [functools.partial(piece, r0, r1) for r0, r1 in cuts(V_TILE, pm, PACK)]

        def grads(y, g):
            return [
                functools.partial(grad_piece, y, g, lab_ref, le_ref, wt_ref, None, start(1), row0, lanes, True, l, r0, r1)
                for l in range(0, t, lanes) for r0, r1 in cuts(V_TILE, pr, PACK)
            ]

        @pl.when(s == 0)
        def _():
            dw_ref[ALL] = in_ref[ALL]
            interleave(logit_pieces(ya), [])

        @pl.when(s == 1)
        def _():
            interleave(logit_pieces(yb), grads(ya, ga))

        for parity, (y_new, y_old, g_new, g_old) in enumerate([(ya, yb, gb, ga), (yb, ya, ga, gb)]):
            @pl.when((s > 1) & (s < last) & (lax.rem(s, 2) == parity))
            def _():
                interleave(alternate(logit_pieces(y_new), out_pieces(g_old)), grads(y_old, g_new))

        y_end, g_end, g_pre = (yb, gb, ga) if last % 2 == 0 else (ya, ga, gb)

        @pl.when(s == last)
        def _():
            interleave(out_pieces(g_pre), grads(y_end, g_end))

        @pl.when(s == last + 1)
        def _():
            interleave(out_pieces(g_end), [])
            whole_ref[ALL] = dw_ref[ALL]

    row = pl.BlockSpec((1, n), lambda s, c: ORIGIN, **once())
    out_blk = pl.BlockSpec((V_TILE, WIDTH), lambda s, c: ORIGIN, **once())
    extra = [] if whole is None else [whole]
    grid_spec = pltpu.PrefetchScalarGridSpec(
        num_scalar_prefetch=1,
        grid=(last + 2,),
        in_specs=[
            pl.BlockSpec((t, WIDTH), lambda s, c: (jnp.minimum(s, last - 1), 0)),
            pl.BlockSpec((t, WIDTH), lambda s, c: (jnp.clip(s - 2, 0, last - 1), 0)),
            pl.BlockSpec((V_TILE, WIDTH), lambda s, c: (c[0] * nv + tile(c), 0), **once()),
            row, row, row, out_blk,
        ] + [pl.BlockSpec(memory_space=pl.ANY)] * len(extra),
        out_specs=[out_blk, pl.BlockSpec((V_TILE, WIDTH), lambda s, c: (c[0] * nv + tile(c), 0), **once())],
        scratch_shapes=[pltpu.VMEM((V_TILE, t), f32)] * TWO + [pltpu.VMEM((V_TILE, t), bf16)] * TWO,
    )
    return pl.pallas_call(
        body,
        grid_spec=grid_spec,
        out_shape=[jax.ShapeDtypeStruct((V_TILE, WIDTH), f32), jax.ShapeDtypeStruct((block, WIDTH), f32)],
        input_output_aliases={SUB: 1} if extra else {},
        compiler_params=params(),
        cost_estimate=cost(2, V_TILE, n, 12 * V_TILE * WIDTH),
        name="other",
    )(meta, feats, feats, out_tab, lab, le, wt, acc, *extra)


def row_sums(order, ids, bounds, parts, before, where, tiles, whole, block):
    m, (n, width) = len(parts), parts[0].shape
    unroll, n_put = PACK, len(tiles)
    has_before = before is not None

    def body(order_ref, id_ref, b_ref, where_ref, *rest):
        rest = list(rest)
        ins = [rest.pop(0) for _ in range(m)]
        put = [rest.pop(0) for _ in range(n_put)]
        if n_put:
            rest.pop(0)
        in_ref = rest.pop(0) if has_before else None
        out_ref = rest.pop(0)
        whole_ref = rest.pop(0) if n_put else None
        buf, sem = rest[:2]
        stage, sem_in, sem_out = rest[2:] if n_put else (None, None, None)
        p = pl.program_id(0)

        def fetch(i):
            return pltpu.make_async_copy(ins[i], buf.at[pl.ds(i * n, n)], sem.at[i])

        @pl.when(p == 0)
        def _():
            for i in range(m):
                fetch(i).start()

        def load(i):
            return pltpu.make_async_copy(put[i], stage.at[i % 2], sem_in.at[i % 2])

        def store(i):
            row = pl.multiple_of(where_ref[i], PACK)
            return pltpu.make_async_copy(stage.at[i % 2], whole_ref.at[pl.ds(row, V_TILE)], sem_out.at[i % 2])

        for i in range(n_put + 2 if n_put else 0):
            @pl.when(p == i)
            def _(i=i):
                if i >= 2:
                    store(i - 2).wait()
                if i < n_put:
                    load(i).start()

        out_ref[ALL] = in_ref[ALL] if has_before else jnp.zeros_like(out_ref)

        @pl.when(p == 0)
        def _():
            for i in range(m):
                fetch(i).wait()

        lo, hi = b_ref[p], b_ref[p + 1]

        def one(k, carry):
            prev, acc = carry
            row, d = order_ref[k], id_ref[k]
            at = pl.ds(d - p * V_TILE, 1)
            x = buf[pl.ds(row, 1), :]
            acc = jnp.where(d == prev, acc + x, (in_ref[at, :] + x) if has_before else x)
            out_ref[at, :] = acc
            return d, acc

        def several(i, carry):
            for u in range(unroll):
                carry = one(lo + i * unroll + u, carry)
            return carry

        full = (hi - lo) // unroll
        carry = lax.fori_loop(0, full, several, (jnp.int32(-1), jnp.zeros((1, width), f32)))
        lax.fori_loop(lo + full * unroll, hi, one, carry)

        for i in range(n_put):
            @pl.when(p == i)
            def _(i=i):
                load(i).wait()
                store(i).start()

    rows = pl.BlockSpec((V_TILE, width), lambda p, *_: (p, 0))
    anywhere = pl.BlockSpec(memory_space=pl.ANY)
    extra = list(tiles) + ([whole] if n_put else []) + ([before] if has_before else [])
    aliases = {4 + m + n_put: 1} if n_put else {}
    if has_before:
        aliases[4 + m + len(extra) - 1] = 0
    grid_spec = pltpu.PrefetchScalarGridSpec(
        num_scalar_prefetch=4,
        grid=(block // V_TILE,),
        in_specs=[anywhere] * (m + n_put + (1 if n_put else 0)) + ([rows] if has_before else []),
        out_specs=[rows] + ([anywhere] if n_put else []),
        scratch_shapes=[pltpu.VMEM((m * n, width), f32), pltpu.SemaphoreType.DMA((m,))] + ([
            pltpu.VMEM((2, V_TILE, width), f32), pltpu.SemaphoreType.DMA((2,)), pltpu.SemaphoreType.DMA((2,))] if n_put else []),
    )
    return pl.pallas_call(
        body,
        grid_spec=grid_spec,
        out_shape=[jax.ShapeDtypeStruct((block, width), f32)] + ([jax.ShapeDtypeStruct(whole.shape, f32)] if n_put else []),
        input_output_aliases=aliases,
        compiler_params=params(),
        cost_estimate=pl.CostEstimate(flops=120_000_000, bytes_accessed=4 * (m * n + block) * width, transcendentals=0),
        name="row_sums",
    )(order, ids, bounds, where, *parts, *extra)


def solution(mesh):
    def local_step(hidden, tokens, emb_blk, out_blk, w_proj, gain_h, gain_e, gain_f):
        batch, piece, width = hidden.shape
        block = emb_blk.shape[0]
        rows = block // TWO
        n_own = batch * piece
        n_c = n_own // N_CHUNK
        tp_rank, cp_rank = lax.axis_index("tp"), lax.axis_index("cp")
        core = lax.rem(cp_rank, 2)
        x_rank = cp_rank // TWO
        meta = jnp.stack([core, x_rank])
        seq_len = piece * 4
        row_start = tp_rank * block + core * rows

        def core_swap(v):
            return lax.ppermute(v, "cp", CORE_SWAP)

        def x_swap(v):
            return lax.ppermute(v, "cp", X_SWAP)

        def y_swap(v):
            return lax.ppermute(v, "tp", Y_SWAP)

        def weights_of(first):
            ranks = cp_rank ^ (first + jnp.arange(2))
            pos = ranks[:, None] * piece + jnp.arange(piece)[None, :]
            w = MTP_WEIGHT * (pos < seq_len - 2).astype(f32)
            return jnp.broadcast_to(w[None, :, None, :], (N_CHUNK, 2, batch // N_CHUNK, piece)).reshape(1, -1)

        head = lax.ppermute(tokens[:, :2], "cp", [(k + 1, k) for k in range(3)])
        ahead = jnp.concatenate([tokens, head], axis=1)
        ids_own = jnp.stack([ahead[:, 1:piece + 1], ahead[:, 2:]]).reshape(2, N_CHUNK, n_c)
        ids_mate = core_swap(ids_own)
        ids_far = x_swap(ids_own)
        ids_diag = core_swap(ids_far)
        next_ids = [v[0] for v in (ids_own, ids_mate, ids_far, ids_diag)]
        labels = [v[1] - row_start for v in (ids_own, ids_mate, ids_far, ids_diag)]
        wt_own, wt_far = weights_of(0), weights_of(2)

        local_next = next_ids[0] - tp_rank * block
        in_block = (local_next >= 0) & (local_next < block)
        take = jnp.clip(local_next, 0, block - 1)
        hid = hidden.reshape(N_CHUNK, n_c, width)

        emb_own, emb_recv = [], []
        for c in range(N_CHUNK):
            e = jnp.where(in_block[c][:, None], jnp.take(emb_blk, take[c], axis=0).astype(f32), 0.0)
            emb_own.append(e)
            emb_recv.append(y_swap(e))

        starts = jnp.arange(block // V_TILE + 1) * V_TILE

        def sorted_ids(chunks):
            ids = jnp.concatenate([next_ids[k][c] for k in (0, 2, 1, 3) for c in chunks]) - tp_rank * block
            seg = jnp.where((ids >= 0) & (ids < block), ids, block)
            seg_sorted, order = lax.sort((seg, jnp.arange(seg.shape[0], dtype=jnp.int32)), num_keys=1)
            bounds = jnp.sum(seg[None, :] < starts[:, None], axis=1).astype(jnp.int32)
            return order, seg_sorted, bounds

        first_ids, last_ids = sorted_ids(range(N_CHUNK - 1)), sorted_ids([N_CHUNK - 1])

        gains = jnp.stack([gain_h, gain_e, gain_f])
        far_parts, f_own, logits, stats = [], None, None, []
        for c in range(N_CHUNK):
            normed = front_kernel(hid[c], emb_own[c], emb_recv[c], w_proj, gains)
            mate = core_swap(normed)
            f_own = round_rows([normed, mate], TWO * n_own, c, f_own)
            far = x_swap(normed)
            far_parts += [far, core_swap(far)]
            logits, st = logits_kernel(meta, out_blk, f_own, rows, c, logits)
            stats.append(st)

        log_sums = ()
        for c in range(N_CHUNK):
            recv = core_swap(stats[c])
            both = merge_halves(stats[c], recv)
            recv = y_swap(both)
            log_sums = finish_stats(both, recv, wt_own, c, log_sums)
        lse_own, le_own = log_sums
        le_far = x_swap(le_own)

        lab_own = jnp.stack(labels[:2], axis=1).reshape(1, -1)
        lab_far = jnp.stack(labels[2:], axis=1).reshape(1, -1)
        own_args = (meta, logits, f_own, out_blk, lab_own, le_own, wt_own)
        f_far = round_rows(far_parts)
        far_args = (meta, f_far, out_blk, lab_far, le_far, wt_far)

        n_kept = rows // V_TILE // TWO
        whole, df_sum, hits, mates = None, None, 0.0, []

        def finish(kept, d_out, whole):
            mine, whole = other_kernel(*far_args, d_out, whole, kept)
            mate = core_swap(mine)
            far = x_swap(mine)
            mates.append((mate, far, core_swap(far)))
            return whole

        for kept in range(n_kept - 1):
            d_out, df_sum, hit = own_kernel(*own_args, kept, None, df_sum, None)
            hits += jnp.sum(wt_own * hit)
            whole = finish(kept, d_out, whole)

        df_terms, d_out = [], None
        for c in range(N_CHUNK):
            d_out, df_own, df_mate, hit = own_kernel(*own_args, n_kept - 1, c, df_sum, d_out)
            hits += jnp.sum(wt_own.reshape(N_CHUNK, 1, -1)[c] * hit)
            recv = core_swap(df_mate)
            mine = df_own + recv
            recv = y_swap(mine)
            df_terms.append((mine, recv))
        whole = finish(n_kept - 1, d_out, whole)

        totals, de_own, de_far, de_mate, de_diag = (), [], [], [], []
        for c in range(N_CHUNK):
            d_hid, de, *sums = back_kernel(hid[c], emb_own[c], emb_recv[c], w_proj, gains, *df_terms[c], c, totals)
            totals = (*sums, d_hid)
            de_own.append(de)
            de_far.append(x_swap(de))
            de_mate.append(core_swap(de))
            de_diag.append(core_swap(de_far[c]))

        mine = (wt_own * lse_own).reshape(N_CHUNK, 2, -1)[:, 0]
        loss_part = 0.5 * jnp.sum(mine) - hits
        d_proj = totals[0]
        small = jnp.concatenate([jnp.sum(totals[1].reshape(3, SUB, width), axis=1), jnp.full((5, width), loss_part)], axis=0)
        half_rows = width // TWO
        mine = lax.dynamic_slice(d_proj, (core * half_rows, 0), (half_rows, TWO * width))
        theirs = lax.dynamic_slice(d_proj, ((1 - core) * half_rows, 0), (half_rows, TWO * width))
        mine, small = mine + core_swap(theirs), small + core_swap(small)
        mine, small = mine + x_swap(mine), small + x_swap(small)
        theirs = core_swap(mine)
        d_proj = lax.dynamic_update_slice(d_proj, mine, (core * half_rows, 0))
        d_proj = lax.dynamic_update_slice(d_proj, theirs, ((1 - core) * half_rows, 0))
        loss_sum = small[3:4, 0] + y_swap(small[3:, :128])[0:1, 0]

        places = []
        for kept in range(n_kept):
            for which, v in enumerate(mates[kept]):
                core_of = core if which == 1 else 1 - core
                x_of = x_rank if which == 0 else 1 - x_rank
                places.append((core_of * rows + (n_kept * x_of + kept) * V_TILE, v))
        early, late = places[:-2], places[-2:]
        kinds = (de_own, de_far, de_mate, de_diag)
        where = jnp.stack([p[0] for p in early])
        d_emb, whole = row_sums(
            *first_ids, [v for kind in kinds for v in kind[:-1]], None, where, [p[1] for p in early], whole, block)
        d_emb, = row_sums(*last_ids, [kind[-1] for kind in kinds], d_emb, where, [], None, block)
        for start, v in late:
            whole = lax.dynamic_update_slice(whole, v, (start, 0))

        loss = LN2 * loss_sum / (batch * (seq_len - 2))
        d_hidden = d_hid.reshape(batch, piece, width)
        return loss, d_hidden, d_proj, d_emb, whole, small[0], small[1], small[2]

    part_seq = P("dp", "cp", None)
    in_specs = (part_seq, P("dp", "cp"), P("tp", None), P("tp", None), P(None, None), P(None), P(None), P(None))
    out_specs = (P("dp"), part_seq, P("dp", None), P(("dp", "tp"), None), P(("dp", "tp"), None), P("dp"), P("dp"), P("dp"))
    return jax.shard_map(local_step, mesh=mesh, in_specs=in_specs, out_specs=out_specs, check_vma=False)
```

time: 1740 us -> 1800 us (1.034)
  waiting for transfers between devices: 469 us -> 647 us
  Pallas kernels: 1070 us -> 948 us
    pallas_call x3, Pallas kernels: 329 us -> 161 us  [other_kernel(): pl.pallas_call(body, grid_spec=grid_spec, out_shape=[jax.ShapeDtypeStruct...]
    ppermute x12 -> x13, waiting for transfers between devices: 231 us -> 371 us  [x_swap(): return lax.ppermute(v, 'cp', X_SWAP)]
    ppermute x10, waiting for transfers between devices: 198 us -> 272 us  [y_swap(): return lax.ppermute(v, 'tp', Y_SWAP)]
    pallas_call x7 -> x8, Pallas kernels: 116 us -> 161 us  [the longest x2 152 us: row_sums(): pl.pallas_call(body, grid_spec=grid_spec, out_shape=[jax.ShapeDtypeStruct...]
    ppermute x25 -> x29, waiting for transfers between devices: 36.3 us -> 0.15 us  [core_swap(): return lax.ppermute(v, 'cp', CORE_SWAP)]
    pallas_call x3 -> x5, Pallas kernels: 335 us -> 338 us  [own_kernel(): pl.pallas_call(body, grid_spec=grid_spec, out_shape=[jax.ShapeDtypeStruct...]
  transfers between devices with their start and end apart: 48 -> 53, of which waited for: 14 -> 13; matrix products, arithmetic and copies ran while one was open for 8% -> 6% of each run, Pallas kernels for 54% -> 50%
where the time goes in v2:
time: 1800 us; the launch traced here: 1790 us
  Pallas kernels  948 us (53%)
  waiting for transfers between devices  647 us (36%)
  local copies, waits for them, and re-layouts  94.4 us (5%)
  other arithmetic  52 us (3%)
  starting transfers between devices  39.2 us (2%)
    ppermute x13, waiting for transfers between devices, x_swap(): return lax.ppermute(v, 'cp', X_SWAP)  371 us
    pallas_call x5, Pallas kernels, own_kernel(): pl.pallas_call(body, grid_spec=grid_spec, out_shape=[jax.ShapeDtypeStruct...  338 us
    ppermute x10, waiting for transfers between devices, y_swap(): return lax.ppermute(v, 'tp', Y_SWAP)  272 us
    pallas_call x3, Pallas kernels, logits_kernel(): pl.pallas_call(body, grid_spec=grid_spec, out_shape=[jax.ShapeDtypeStruct...  190 us
    pallas_call x3, Pallas kernels, other_kernel(): pl.pallas_call(body, grid_spec=grid_spec, out_shape=[jax.ShapeDtypeStruct...  161 us
    pallas_call x2, Pallas kernels, row_sums(): pl.pallas_call(body, grid_spec=grid_spec, out_shape=[jax.ShapeDtypeStruct...  152 us
    gather x3, local copies, waits for them, and re-layouts, local_step(): jnp.take(emb_blk, take[c], axis=0).astype(f32)  51.8 us
    pallas_call x3, Pallas kernels, back_kernel(): pl.pallas_call(body, grid=(n // tile,), in_specs=tiles_of(tile, width, wi...  42.9 us
  transfers between devices with their start and end apart: 53, of which 13 were waited for; matrix products, arithmetic and copies ran while one was open for 6% of the time, Pallas kernels for 50%

profile of v2, /device:TPU:1, one launch (start us, length us, event | category | flops | bytes accessed | tf_op | source)
XLA Modules:
  0.0 1788.6 jit_solution(6259997270849553738)
XLA Ops:
  1.3 1.9 collective-permute-start
  3.3 3.9 collective-permute-done
  8.9 17.6 gather_fusion.2
  26.5 2.5 convert_select_fusion.own_ref
  31.0 4.7 fusion.9
  35.7 17.1 gather_fusion
  52.9 17.1 gather_fusion.1
  70.2 3.8 convert_select_fusion.1.own_ref
  74.5 2.6 convert_select_fusion.2.own_ref
  78.1 21.3 %collective-permute-done.5.recv_ref = f32[1536,512]{1,0:T(8,128)} collective-permute-done((f32[1536,512]{1,0:T(8,128)S(1)}, f32[1536,512]{1,0:T(8,128)}, u32[]{:S(2)}, u32[]{:S(2)}) %collective-permute-start.5) | collective-permute-done | bytes 3145760 | tf_op jit(solution)/shard_map/ppermute | solution.py:682
  99.3 7.7 front.5.refs_0_
  114.9 51.9 %collective-permute-done.3.recv_ref = f32[1536,512]{1,0:T(8,128)} collective-permute-done((f32[1536,512]{1,0:T(8,128)}, f32[1536,512]{1,0:T(8,128)}, u32[]{:S(2)}, u32[]{:S(2)}) %collective-permute-start.3) | collective-permute-done | bytes 3145760 | tf_op jit(solution)/shard_map/ppermute | solution.py:682
  166.8 7.6 front.4.refs_0_
  174.4 58.2 %collective-permute-done.1.recv_ref = f32[1536,512]{1,0:T(8,128)} collective-permute-done((f32[1536,512]{1,0:T(8,128)}, f32[1536,512]{1,0:T(8,128)}, u32[]{:S(2)}, u32[]{:S(2)}) %collective-permute-start.1) | collective-permute-done | bytes 3145760 | tf_op jit(solution)/shard_map/ppermute | solution.py:682
  232.5 7.6 front.3.refs_0_
  240.2 5.6 round_rows.4.refs_2_.f_ref
  245.7 63.2 %logits.3 = (f32[12576,9216]{1,0:T(8,128)}, f32[2,3072]{1,0:T(2,128)}) custom-call(s32[2]{0:T(128)} %pad_add_fusion.4.meta_ref, bf16[25152,512]{1,0:T(8,128)(2,1)} %w_ref.33, bf16[9216,512]{1,0:T(8,128)(2,1)} %round_rows.4.refs_2_.f_ref), custom_call_target="tpu_custom_call" | custom-call | flops 39560675328 | bytes 154533888 | tf_op jit(solution)/shard_map/logits/pallas_call | solution.py:319
  308.9 5.6 round_rows.5.refs_2_.f_ref
  314.5 63.4 %logits.4 = (f32[12576,9216]{1,0:T(8,128)}, f32[2,3072]{1,0:T(2,128)}) custom-call(s32[2]{0:T(128)} %pad_add_fusion.4.meta_ref, bf16[25152,512]{1,0:T(8,128)(2,1)} %w_ref.33, bf16[9216,512]{1,0:T(8,128)(2,1)} %round_rows.5.refs_2_.f_ref, f32[12576,9216]{1,0:T(8,128)} %get-tuple-element.63.rest_0_), custom_call_target="tpu_custom_call", output_to_operand_aliasing={{0}: (3, {})} | custom-call | flops 39560675328 | bytes 154533888 | tf_op jit(solution)/shard_map/logits/pallas_call | solution.py:319
  377.9 5.5 round_rows.6.f_ref
  383.4 63.2 %logits.5 = (f32[12576,9216]{1,0:T(8,128)}, f32[2,3072]{1,0:T(2,128)}) custom-call(s32[2]{0:T(128)} %pad_add_fusion.4.meta_ref, bf16[25152,512]{1,0:T(8,128)(2,1)} %w_ref.33, bf16[9216,512]{1,0:T(8,128)(2,1)} %round_rows.6.f_ref, f32[12576,9216]{1,0:T(8,128)} %get-tuple-element.64.rest_0_), custom_call_target="tpu_custom_call", output_to_operand_aliasing={{0}: (3, {})} | custom-call | flops 39560675328 | bytes 154533888 | tf_op jit(solution)/shard_map/logits/pallas_call | solution.py:319
  449.0 1.4 merge_halves.3.a_ref
  450.4 1.7 collective-permute-start.9
  452.8 1.4 merge_halves.4.a_ref
  454.8 1.4 merge_halves.5.a_ref
  456.2 1.5 collective-permute-start.13
  463.9 1.4 finish_stats.4
  467.4 62.0 %own.5 = (f32[2096,512]{1,0:T(8,128)}, f32[3,2,512,1536]{3,2,1,0:T(8,128)}, f32[16,9216]{1,0:T(8,128)}) custom-call(s32[2]{0:T(128)} %pad_add_fusion.4.meta_ref, f32[12576,9216]{1,0:T(8,128)} %get-tuple-element.65.y_ref, bf16[9216,512]{1,0:T(8,128)(2,1)} %round_rows.6.f_ref, bf16[25152,512]{1,0:T(8,128)(2,1)} %w_ref.33, s32[1,9216]{1,0:T(1,128)} %reshape.334.lab_ref, ...), custom_call_target="tpu_custom_call" | custom-call | flops 39560675328 | bytes 77266944 | tf_op jit(solution)/shard_map/own/pallas_call | solution.py:463
  529.3 64.3 %own.6 = (f32[2096,512]{1,0:T(8,128)}, f32[3,2,512,1536]{3,2,1,0:T(8,128)}, f32[16,9216]{1,0:T(8,128)}) custom-call(s32[2]{0:T(128)} %pad_add_fusion.4.meta_ref, f32[12576,9216]{1,0:T(8,128)} %get-tuple-element.65.y_ref, bf16[9216,512]{1,0:T(8,128)(2,1)} %round_rows.6.f_ref, bf16[25152,512]{1,0:T(8,128)(2,1)} %w_ref.33, s32[1,9216]{1,0:T(1,128)} %reshape.334.lab_ref, ...), custom_call_target="tpu_custom_call" | custom-call | flops 39560675328 | bytes 77266944 | tf_op jit(solution)/shard_map/own/pallas_call | solution.py:463
  593.6 65.7 %own.7 = (f32[2096,512]{1,0:T(8,128)}, f32[512,1536]{1,0:T(8,128)}, f32[512,1536]{1,0:T(8,128)}, f32[16,3072]{1,0:T(8,128)}) custom-call(s32[2]{0:T(128)} %pad_add_fusion.4.meta_ref, f32[12576,9216]{1,0:T(8,128)} %get-tuple-element.65.y_ref, bf16[9216,512]{1,0:T(8,128)(2,1)} %round_rows.6.f_ref, bf16[25152,512]{1,0:T(8,128)(2,1)} %w_ref.33, ...), custom_call_target="tpu_custom_call" | custom-call | flops 52747567104 | bytes 103022592 | tf_op jit(solution)/shard_map/own/pallas_call | solution.py:463
  659.3 79.3 %own.8 = (f32[2096,512]{1,0:T(8,128)}, f32[512,1536]{1,0:T(8,128)}, f32[512,1536]{1,0:T(8,128)}, f32[16,3072]{1,0:T(8,128)}) custom-call(s32[2]{0:T(128)} %pad_add_fusion.4.meta_ref, f32[12576,9216]{1,0:T(8,128)} %get-tuple-element.65.y_ref, bf16[9216,512]{1,0:T(8,128)(2,1)} %round_rows.6.f_ref, bf16[25152,512]{1,0:T(8,128)(2,1)} %w_ref.33, ...), custom_call_target="tpu_custom_call" | custom-call | flops 52747567104 | bytes 103022592 | tf_op jit(solution)/shard_map/own/pallas_call | solution.py:463
  739.6 67.2 %own.9 = (f32[2096,512]{1,0:T(8,128)}, f32[512,1536]{1,0:T(8,128)}, f32[512,1536]{1,0:T(8,128)}, f32[16,3072]{1,0:T(8,128)}) custom-call(s32[2]{0:T(128)} %pad_add_fusion.4.meta_ref, f32[12576,9216]{1,0:T(8,128)} %get-tuple-element.65.y_ref, bf16[9216,512]{1,0:T(8,128)(2,1)} %round_rows.6.f_ref, bf16[25152,512]{1,0:T(8,128)(2,1)} %w_ref.33, ...), custom_call_target="tpu_custom_call" | custom-call | flops 52747567104 | bytes 103022592 | tf_op jit(solution)/shard_map/own/pallas_call | solution.py:463
  807.4 5.2 add.151.a_ref
  814.2 4.4 add.150.a_ref
  819.0 2.2 add.149.a_ref
  832.9 15.8 round_rows.7.f_ref.fl_ref
  848.7 33.9 %collective-permute-done.19.b_ref = f32[512,1536]{1,0:T(8,128)} collective-permute-done((f32[512,1536]{1,0:T(8,128)}, f32[512,1536]{1,0:T(8,128)}, u32[]{:S(2)}, u32[]{:S(2)}) %collective-permute-start.19) | collective-permute-done | bytes 3145760 | tf_op jit(solution)/shard_map/ppermute | solution.py:682
  882.6 13.9 back.3
  896.5 53.5 %collective-permute-done.17.b_ref = f32[512,1536]{1,0:T(8,128)} collective-permute-done((f32[512,1536]{1,0:T(8,128)}, f32[512,1536]{1,0:T(8,128)}, u32[]{:S(2)}, u32[]{:S(2)}) %collective-permute-start.17) | collective-permute-done | bytes 3145760 | tf_op jit(solution)/shard_map/ppermute | solution.py:682
  950.0 14.5 back.4
  964.5 52.9 %collective-permute-done.15.b_ref = f32[512,1536]{1,0:T(8,128)} collective-permute-done((f32[512,1536]{1,0:T(8,128)}, f32[512,1536]{1,0:T(8,128)}, u32[]{:S(2)}, u32[]{:S(2)}) %collective-permute-start.15) | collective-permute-done | bytes 3145760 | tf_op jit(solution)/shard_map/ppermute | solution.py:682
  1017.4 14.4 back.5
  1035.2 53.9 %other.3 = (f32[2096,512]{1,0:T(8,128)}, f32[25152,512]{1,0:T(8,128)}) custom-call(s32[2]{0:T(128)} %pad_add_fusion.4.meta_ref, bf16[9216,512]{1,0:T(8,128)(2,1)} %round_rows.7.f_ref.fl_ref, bf16[9216,512]{1,0:T(8,128)(2,1)} %round_rows.7.f_ref.fl_ref, bf16[25152,512]{1,0:T(8,128)(2,1)} %w_ref.33, s32[1,9216]{1,0:T(1,128)} %reshape.339.lab_ref, ...), custom_call_target="tpu_custom_call" | custom-call | flops 39560675328 | bytes 12877824 | tf_op jit(solution)/shard_map/other/pallas_call | solution.py:551
  1091.9 53.7 %other.4 = (f32[2096,512]{1,0:T(8,128)}, f32[25152,512]{1,0:T(8,128)}) custom-call(s32[2]{0:T(128)} %pad_add_fusion.4.meta_ref, bf16[9216,512]{1,0:T(8,128)(2,1)} %round_rows.7.f_ref.fl_ref, bf16[9216,512]{1,0:T(8,128)(2,1)} %round_rows.7.f_ref.fl_ref, bf16[25152,512]{1,0:T(8,128)(2,1)} %w_ref.33, ...), custom_call_target="tpu_custom_call", output_to_operand_aliasing={{1}: (8, {})} | custom-call | flops 39560675328 | bytes 12877824 | tf_op jit(solution)/shard_map/other/pallas_call | solution.py:551
  1147.6 35.9 %collective-permute-done.21 = f32[8,512]{1,0:T(8,128)} collective-permute-done((f32[8,512]{1,0:T(8,128)}, f32[8,512]{1,0:T(8,128)}, u32[]{:S(2)}, u32[]{:S(2)}) %collective-permute-start.21) | collective-permute-done | bytes 16416 | tf_op jit(solution)/shard_map/ppermute | solution.py:679
  1186.1 2.3 constant_dynamic-slice_fusion
  1189.0 2.5 collective-permute-start.23
  1191.5 53.5 %other.5 = (f32[2096,512]{1,0:T(8,128)}, f32[25152,512]{1,0:T(8,128)}) custom-call(s32[2]{0:T(128)} %pad_add_fusion.4.meta_ref, bf16[9216,512]{1,0:T(8,128)(2,1)} %round_rows.7.f_ref.fl_ref, bf16[9216,512]{1,0:T(8,128)(2,1)} %round_rows.7.f_ref.fl_ref, bf16[25152,512]{1,0:T(8,128)(2,1)} %w_ref.33, ...), custom_call_target="tpu_custom_call", output_to_operand_aliasing={{1}: (8, {})} | custom-call | flops 39560675328 | bytes 12877824 | tf_op jit(solution)/shard_map/other/pallas_call | solution.py:551
  1247.6 1.7 dynamic-slice_add_fusion
  1249.3 26.3 %collective-permute-done.48.rest_12_ = f32[2096,512]{1,0:T(8,128)} collective-permute-done((f32[2096,512]{1,0:T(8,128)}, f32[2096,512]{1,0:T(8,128)}, u32[]{:S(2)}, u32[]{:S(2)}) %collective-permute-start.48) | collective-permute-done | bytes 4292640 | tf_op jit(solution)/shard_map/ppermute | solution.py:679
  1277.0 90.5 %collective-permute-done.51 = f32[2096,512]{1,0:T(8,128)} collective-permute-done((f32[2096,512]{1,0:T(8,128)}, f32[2096,512]{1,0:T(8,128)}, u32[]{:S(2)}, u32[]{:S(2)}) %collective-permute-start.51) | collective-permute-done | bytes 4292640 | tf_op jit(solution)/shard_map/ppermute | solution.py:679
  1367.6 2.3 collective-permute-start.33
  1369.8 154.9 %collective-permute-done.24 = f32[256,1024]{1,0:T(8,128)S(1)} collective-permute-done((f32[256,1024]{1,0:T(8,128)S(1)}, f32[256,1024]{1,0:T(8,128)S(1)}, u32[]{:S(2)}, u32[]{:S(2)}) %collective-permute-start.24) | collective-permute-done | bytes 1048608 | tf_op jit(solution)/shard_map/ppermute | solution.py:679
  1524.7 2.3 collective-permute-start.46
  1528.7 63.6 %collective-permute-done.32.rest_3_ = f32[1536,512]{1,0:T(8,128)} collective-permute-done((f32[1536,512]{1,0:T(8,128)}, f32[1536,512]{1,0:T(8,128)}, u32[]{:S(2)}, u32[]{:S(2)}) %collective-permute-start.32) | collective-permute-done | bytes 3145760 | tf_op jit(solution)/shard_map/ppermute | solution.py:679
  1593.6 1.7 copy-done.4
  1601.5 6.8 sort.30
  1608.3 8.2 sort.31
  1619.3 1.4 fusion.11
  1623.2 2.3 constant_dynamic-update-slice_fusion.12
  1625.6 90.1 %row_sums.2 = (f32[25152,512]{1,0:T(8,128)}, f32[25152,512]{1,0:T(8,128)}) custom-call(s32[12288]{0:T(1024)} %get-tuple-element.102.order_ref, s32[12288]{0:T(1024)} %get-tuple-element.103.id_ref, s32[13]{0:T(128)} %convert_reduce_fusion.b_ref, s32[7]{0:T(128)} %stack.82.where_ref, ...), custom_call_target="tpu_custom_call", output_to_operand_aliasing={{1}: (19, {})} | custom-call | flops 120000000 | bytes 76677120 | tf_op jit(solution)/shard_map/row_sums/pallas_call | solution.py:650
  1715.6 4.7 constant_dynamic-update-slice_fusion.11
  1720.4 4.7 constant_dynamic-update-slice_fusion.10
  1725.1 62.2 %row_sums.3 = f32[25152,512]{1,0:T(8,128)} custom-call(s32[6144]{0:T(1024)} %get-tuple-element.99.order_ref, s32[6144]{0:T(1024)} %get-tuple-element.100.id_ref, s32[13]{0:T(128)} %convert_reduce_fusion.1.b_ref, s32[7]{0:T(128)} %stack.82.where_ref, f32[1536,512]{1,0:T(8,128)} %get-tuple-element.101.rest_0_, ...), custom_call_target="tpu_custom_call", output_to_operand_aliasing={{}: (8, {})} | custom-call | flops 120000000 | bytes 64094208 | tf_op jit(solution)/shard_map/row_sums/pallas_call | solution.py:650
  (242 shorter events, 65.4 us)
Async XLA Ops:
  1.3 5.9 collective-permute-start
  29.1 70.2 %collective-permute-start.5 = (f32[1536,512]{1,0:T(8,128)S(1)}, f32[1536,512]{1,0:T(8,128)}, u32[]{:S(2)}, u32[]{:S(2)}) collective-permute-start(f32[1536,512]{1,0:T(8,128)S(1)} %convert_select_fusion.own_ref), channel_id=1, source_target_pairs={{0,4},{4,0},{1,5},{5,1},{2,6},{6,2},{3,7},{7,3}} | collective-permute-start | bytes 9437192 | tf_op jit(solution)/shard_map/ppermute | solution.py:682
  74.0 92.8 %collective-permute-start.3 = (f32[1536,512]{1,0:T(8,128)}, f32[1536,512]{1,0:T(8,128)}, u32[]{:S(2)}, u32[]{:S(2)}) collective-permute-start(f32[1536,512]{1,0:T(8,128)} %convert_select_fusion.1.own_ref), channel_id=1, source_target_pairs={{0,4},{4,0},{1,5},{5,1},{2,6},{6,2},{3,7},{7,3}} | collective-permute-start | bytes 9437192 | tf_op jit(solution)/shard_map/ppermute | solution.py:682
  77.1 155.5 %collective-permute-start.1 = (f32[1536,512]{1,0:T(8,128)}, f32[1536,512]{1,0:T(8,128)}, u32[]{:S(2)}, u32[]{:S(2)}) collective-permute-start(f32[1536,512]{1,0:T(8,128)} %convert_select_fusion.2.own_ref), channel_id=1, source_target_pairs={{0,4},{4,0},{1,5},{5,1},{2,6},{6,2},{3,7},{7,3}} | collective-permute-start | bytes 9437192 | tf_op jit(solution)/shard_map/ppermute | solution.py:682
  107.1 133.1 %collective-permute-start.6 = (f32[1536,512]{1,0:T(8,128)}, f32[1536,512]{1,0:T(8,128)}, u32[]{:S(2)}, u32[]{:S(2)}) collective-permute-start(f32[1536,512]{1,0:T(8,128)} %front.5.refs_0_), channel_id=1, source_target_pairs={{0,1},{1,0},{2,3},{3,2},{4,5},{5,4},{6,7},{7,6}} | collective-permute-start | bytes 9437192 | tf_op jit(solution)/shard_map/ppermute | solution.py:676
  113.2 334.5 %collective-permute-start.7 = (s32[2,3,1536]{2,1,0:T(4,128)}, s32[2,3,1536]{2,1,0:T(4,128)}, u32[]{:S(2)}, u32[]{:S(2)}) collective-permute-start(s32[2,3,1536]{2,1,0:T(4,128)} %constant_dynamic-update-slice_fusion), channel_id=1, source_target_pairs={{0,1},{1,0},{2,3},{3,2},{4,5},{5,4},{6,7},{7,6}} | collective-permute-start | bytes 110600 | tf_op jit(solution)/shard_map/ppermute | solution.py:676
  113.7 345.4 %collective-permute-start.26 = (s32[2,3,1536]{2,1,0:T(4,128)}, s32[2,3,1536]{2,1,0:T(4,128)}, u32[]{:S(2)}, u32[]{:S(2)}) collective-permute-start(s32[2,3,1536]{2,1,0:T(4,128)} %constant_dynamic-update-slice_fusion), channel_id=1, source_target_pairs={{0,2},{2,0},{1,3},{3,1},{4,6},{6,4},{5,7},{7,5}} | collective-permute-start | bytes 110600 | tf_op jit(solution)/shard_map/ppermute | solution.py:679
  174.4 134.6 %collective-permute-start.4 = (f32[1536,512]{1,0:T(8,128)}, f32[1536,512]{1,0:T(8,128)}, u32[]{:S(2)}, u32[]{:S(2)}) collective-permute-start(f32[1536,512]{1,0:T(8,128)} %front.4.refs_0_), channel_id=1, source_target_pairs={{0,1},{1,0},{2,3},{3,2},{4,5},{5,4},{6,7},{7,6}} | collective-permute-start | bytes 9437192 | tf_op jit(solution)/shard_map/ppermute | solution.py:676
  240.2 137.7 %collective-permute-start.2 = (f32[1536,512]{1,0:T(8,128)}, f32[1536,512]{1,0:T(8,128)}, u32[]{:S(2)}, u32[]{:S(2)}) collective-permute-start(f32[1536,512]{1,0:T(8,128)} %front.3.refs_0_), channel_id=1, source_target_pairs={{0,1},{1,0},{2,3},{3,2},{4,5},{5,4},{6,7},{7,6}} | collective-permute-start | bytes 9437192 | tf_op jit(solution)/shard_map/ppermute | solution.py:676
  446.6 1.8 collective-permute-start.8
  447.2 5.0 collective-permute-start.10
  447.2 7.0 collective-permute-start.12
  450.4 14.9 collective-permute-start.9
  454.2 8.8 collective-permute-start.11
  456.2 4.8 collective-permute-start.13
  459.2 280.4 %collective-permute-start.27 = (s32[2,3,1536]{2,1,0:T(4,128)}, s32[2,3,1536]{2,1,0:T(4,128)}, u32[]{:S(2)}, u32[]{:S(2)}) collective-permute-start(s32[2,3,1536]{2,1,0:T(4,128)} %collective-permute-done.26), channel_id=1, source_target_pairs={{0,1},{1,0},{2,3},{3,2},{4,5},{5,4},{6,7},{7,6}} | collective-permute-start | bytes 110600 | tf_op jit(solution)/shard_map/ppermute | solution.py:676
  460.1 346.7 %collective-permute-start.37 = (f32[1536,512]{1,0:T(8,128)}, f32[1536,512]{1,0:T(8,128)}, u32[]{:S(2)}, u32[]{:S(2)}) collective-permute-start(f32[1536,512]{1,0:T(8,128)} %front.5.refs_0_), channel_id=1, source_target_pairs={{0,2},{2,0},{1,3},{3,1},{4,6},{6,4},{5,7},{7,5}} | collective-permute-start | bytes 9437192 | tf_op jit(solution)/shard_map/ppermute | solution.py:679
  461.0 351.5 %collective-permute-start.39 = (f32[1536,512]{1,0:T(8,128)}, f32[1536,512]{1,0:T(8,128)}, u32[]{:S(2)}, u32[]{:S(2)}) collective-permute-start(f32[1536,512]{1,0:T(8,128)} %front.4.refs_0_), channel_id=1, source_target_pairs={{0,2},{2,0},{1,3},{3,1},{4,6},{6,4},{5,7},{7,5}} | collective-permute-start | bytes 9437192 | tf_op jit(solution)/shard_map/ppermute | solution.py:679
  463.1 350.0 %collective-permute-start.41 = (f32[1536,512]{1,0:T(8,128)}, f32[1536,512]{1,0:T(8,128)}, u32[]{:S(2)}, u32[]{:S(2)}) collective-permute-start(f32[1536,512]{1,0:T(8,128)} %front.3.refs_0_), channel_id=1, source_target_pairs={{0,2},{2,0},{1,3},{3,1},{4,6},{6,4},{5,7},{7,5}} | collective-permute-start | bytes 9437192 | tf_op jit(solution)/shard_map/ppermute | solution.py:679
  738.6 74.5 %collective-permute-start.16 = (f32[512,1536]{1,0:T(8,128)}, f32[512,1536]{1,0:T(8,128)}, u32[]{:S(2)}, u32[]{:S(2)}) collective-permute-start(f32[512,1536]{1,0:T(8,128)} %get-tuple-element.81), channel_id=1, source_target_pairs={{0,1},{1,0},{2,3},{3,2},{4,5},{5,4},{6,7},{7,6}} | collective-permute-start | bytes 9437192 | tf_op jit(solution)/shard_map/ppermute | solution.py:676
  739.5 67.8 %collective-permute-start.18 = (f32[512,1536]{1,0:T(8,128)}, f32[512,1536]{1,0:T(8,128)}, u32[]{:S(2)}, u32[]{:S(2)}) collective-permute-start(f32[512,1536]{1,0:T(8,128)} %get-tuple-element.83), channel_id=1, source_target_pairs={{0,1},{1,0},{2,3},{3,2},{4,5},{5,4},{6,7},{7,6}} | collective-permute-start | bytes 9437192 | tf_op jit(solution)/shard_map/ppermute | solution.py:676
  806.8 11.8 collective-permute-start.14
  807.3 14.0 collective-permute-start.38
  807.3 6.9 copy-start.5
  812.6 19.3 %collective-permute-start.40 = (f32[1536,512]{1,0:T(8,128)}, f32[1536,512]{1,0:T(8,128)}, u32[]{:S(2)}, u32[]{:S(2)}) collective-permute-start(f32[1536,512]{1,0:T(8,128)} %collective-permute-done.39.refs_2_), channel_id=1, source_target_pairs={{0,1},{1,0},{2,3},{3,2},{4,5},{5,4},{6,7},{7,6}} | collective-permute-start | bytes 9437192 | tf_op jit(solution)/shard_map/ppermute | solution.py:676
  813.0 19.9 %collective-permute-start.42 = (f32[1536,512]{1,0:T(8,128)}, f32[1536,512]{1,0:T(8,128)}, u32[]{:S(2)}, u32[]{:S(2)}) collective-permute-start(f32[1536,512]{1,0:T(8,128)} %collective-permute-done.41.refs_4_), channel_id=1, source_target_pairs={{0,1},{1,0},{2,3},{3,2},{4,5},{5,4},{6,7},{7,6}} | collective-permute-start | bytes 9437192 | tf_op jit(solution)/shard_map/ppermute | solution.py:676
  813.1 69.5 %collective-permute-start.19 = (f32[512,1536]{1,0:T(8,128)}, f32[512,1536]{1,0:T(8,128)}, u32[]{:S(2)}, u32[]{:S(2)}) collective-permute-start(f32[512,1536]{1,0:T(8,128)} %add.151.a_ref), channel_id=1, source_target_pairs={{0,4},{4,0},{1,5},{5,1},{2,6},{6,2},{3,7},{7,3}} | collective-permute-start | bytes 9437192 | tf_op jit(solution)/shard_map/ppermute | solution.py:682
  818.6 131.4 %collective-permute-start.17 = (f32[512,1536]{1,0:T(8,128)}, f32[512,1536]{1,0:T(8,128)}, u32[]{:S(2)}, u32[]{:S(2)}) collective-permute-start(f32[512,1536]{1,0:T(8,128)} %add.150.a_ref), channel_id=1, source_target_pairs={{0,4},{4,0},{1,5},{5,1},{2,6},{6,2},{3,7},{7,3}} | collective-permute-start | bytes 9437192 | tf_op jit(solution)/shard_map/ppermute | solution.py:682
  818.9 6.7 copy-start.2
  818.9 6.6 copy-start.12
  818.9 8.1 copy-start.8
  819.0 8.1 copy-start.9
  819.0 10.2 copy-start.15
  819.0 10.2 copy-start.16
  819.0 10.2 copy-start.17
  821.2 196.2 %collective-permute-start.15 = (f32[512,1536]{1,0:T(8,128)}, f32[512,1536]{1,0:T(8,128)}, u32[]{:S(2)}, u32[]{:S(2)}) collective-permute-start(f32[512,1536]{1,0:T(8,128)} %add.149.a_ref), channel_id=1, source_target_pairs={{0,4},{4,0},{1,5},{5,1},{2,6},{6,2},{3,7},{7,3}} | collective-permute-start | bytes 9437192 | tf_op jit(solution)/shard_map/ppermute | solution.py:682
  831.8 203.4 %collective-permute-start.43 = (f32[1,9216]{1,0:T(1,128)}, f32[1,9216]{1,0:T(1,128)}, u32[]{:S(2)}, u32[]{:S(2)}) collective-permute-start(f32[1,9216]{1,0:T(1,128)} %get-tuple-element.73.le_ref), channel_id=1, source_target_pairs={{0,2},{2,0},{1,3},{3,1},{4,6},{6,4},{5,7},{7,5}} | collective-permute-start | bytes 110600 | tf_op jit(solution)/shard_map/ppermute | solution.py:679
  1033.9 56.2 %collective-permute-start.20 = (f32[8,512]{1,0:T(8,128)}, f32[8,512]{1,0:T(8,128)}, u32[]{:S(2)}, u32[]{:S(2)}) collective-permute-start(f32[8,512]{1,0:T(8,128)} %concatenate.22), channel_id=1, source_target_pairs={{0,1},{1,0},{2,3},{3,2},{4,5},{5,4},{6,7},{7,6}} | collective-permute-start | bytes 49160 | tf_op jit(solution)/shard_map/ppermute | solution.py:676
  1089.1 155.9 %collective-permute-start.44 = (f32[2096,512]{1,0:T(8,128)}, f32[2096,512]{1,0:T(8,128)}, u32[]{:S(2)}, u32[]{:S(2)}) collective-permute-start(f32[2096,512]{1,0:T(8,128)} %get-tuple-element.107), channel_id=1, source_target_pairs={{0,1},{1,0},{2,3},{3,2},{4,5},{5,4},{6,7},{7,6}} | collective-permute-start | bytes 12877832 | tf_op jit(solution)/shard_map/ppermute | solution.py:676
  1089.1 156.9 %collective-permute-start.45 = (f32[2096,512]{1,0:T(8,128)}, f32[2096,512]{1,0:T(8,128)}, u32[]{:S(2)}, u32[]{:S(2)}) collective-permute-start(f32[2096,512]{1,0:T(8,128)} %get-tuple-element.107), channel_id=1, source_target_pairs={{0,2},{2,0},{1,3},{3,1},{4,6},{6,4},{5,7},{7,5}} | collective-permute-start | bytes 12877832 | tf_op jit(solution)/shard_map/ppermute | solution.py:679
  1091.4 92.1 %collective-permute-start.21 = (f32[8,512]{1,0:T(8,128)}, f32[8,512]{1,0:T(8,128)}, u32[]{:S(2)}, u32[]{:S(2)}) collective-permute-start(f32[8,512]{1,0:T(8,128)} %pad_add_fusion.3), channel_id=1, source_target_pairs={{0,2},{2,0},{1,3},{3,1},{4,6},{6,4},{5,7},{7,5}} | collective-permute-start | bytes 49160 | tf_op jit(solution)/shard_map/ppermute | solution.py:679
  1145.6 100.9 %collective-permute-start.47 = (f32[2096,512]{1,0:T(8,128)}, f32[2096,512]{1,0:T(8,128)}, u32[]{:S(2)}, u32[]{:S(2)}) collective-permute-start(f32[2096,512]{1,0:T(8,128)} %get-tuple-element.110), channel_id=1, source_target_pairs={{0,1},{1,0},{2,3},{3,2},{4,5},{5,4},{6,7},{7,6}} | collective-permute-start | bytes 12877832 | tf_op jit(solution)/shard_map/ppermute | solution.py:676
  1146.7 128.9 %collective-permute-start.48 = (f32[2096,512]{1,0:T(8,128)}, f32[2096,512]{1,0:T(8,128)}, u32[]{:S(2)}, u32[]{:S(2)}) collective-permute-start(f32[2096,512]{1,0:T(8,128)} %get-tuple-element.110), channel_id=1, source_target_pairs={{0,2},{2,0},{1,3},{3,1},{4,6},{6,4},{5,7},{7,5}} | collective-permute-start | bytes 12877832 | tf_op jit(solution)/shard_map/ppermute | solution.py:679
  1184.9 3.4 collective-permute-start.22
  1189.0 56.0 %collective-permute-start.23 = (f32[256,1024]{1,0:T(8,128)}, f32[256,1024]{1,0:T(8,128)}, u32[]{:S(2)}, u32[]{:S(2)}) collective-permute-start(f32[256,1024]{1,0:T(8,128)} %constant_dynamic-slice_fusion), channel_id=1, source_target_pairs={{0,1},{1,0},{2,3},{3,2},{4,5},{5,4},{6,7},{7,6}} | collective-permute-start | bytes 3145736 | tf_op jit(solution)/shard_map/ppermute | solution.py:676
  1244.9 122.6 %copy-start.3 = (f32[1536,512]{1,0:T(8,128)S(1)}, f32[1536,512]{1,0:T(8,128)}, u32[]{:S(2)}) copy-start(f32[1536,512]{1,0:T(8,128)} %get-tuple-element.104.rest_0_) | copy-start | bytes 9437188
  1245.0 31.6 %collective-permute-start.50 = (f32[2096,512]{1,0:T(8,128)}, f32[2096,512]{1,0:T(8,128)}, u32[]{:S(2)}, u32[]{:S(2)}) collective-permute-start(f32[2096,512]{1,0:T(8,128)} %get-tuple-element.113), channel_id=1, source_target_pairs={{0,1},{1,0},{2,3},{3,2},{4,5},{5,4},{6,7},{7,6}} | collective-permute-start | bytes 12877832 | tf_op jit(solution)/shard_map/ppermute | solution.py:676
  1245.0 122.5 %collective-permute-start.51 = (f32[2096,512]{1,0:T(8,128)}, f32[2096,512]{1,0:T(8,128)}, u32[]{:S(2)}, u32[]{:S(2)}) collective-permute-start(f32[2096,512]{1,0:T(8,128)} %get-tuple-element.113), channel_id=1, source_target_pairs={{0,2},{2,0},{1,3},{3,1},{4,6},{6,4},{5,7},{7,5}} | collective-permute-start | bytes 12877832 | tf_op jit(solution)/shard_map/ppermute | solution.py:679
  1246.1 280.9 %collective-permute-start.28 = (f32[1536,512]{1,0:T(8,128)}, f32[1536,512]{1,0:T(8,128)}, u32[]{:S(2)}, u32[]{:S(2)}) collective-permute-start(f32[1536,512]{1,0:T(8,128)} %get-tuple-element.101.rest_0_), channel_id=1, source_target_pairs={{0,2},{2,0},{1,3},{3,1},{4,6},{6,4},{5,7},{7,5}} | collective-permute-start | bytes 9437192 | tf_op jit(solution)/shard_map/ppermute | solution.py:679
  1246.5 280.5 %collective-permute-start.31 = (f32[1536,512]{1,0:T(8,128)}, f32[1536,512]{1,0:T(8,128)}, u32[]{:S(2)}, u32[]{:S(2)}) collective-permute-start(f32[1536,512]{1,0:T(8,128)} %get-tuple-element.104.rest_0_), channel_id=1, source_target_pairs={{0,2},{2,0},{1,3},{3,1},{4,6},{6,4},{5,7},{7,5}} | collective-permute-start | bytes 9437192 | tf_op jit(solution)/shard_map/ppermute | solution.py:679
  1247.6 350.3 %copy-start.13 = (s32[24,192]{1,0:T(8,128)S(1)}, s32[24,192]{1,0:T(8,128)}, u32[]{:S(2)}) copy-start(s32[24,192]{1,0:T(8,128)} %param.11) | copy-start | bytes 55300
  1247.6 350.3 %copy-start.19 = (s32[24,2]{1,0:T(8,128)S(1)}, s32[24,2]{1,0:T(8,128)}, u32[]{:S(2)}) copy-start(s32[24,2]{1,0:T(8,128)} %copy-done.18) | copy-start | bytes 580
  1275.6 249.2 %collective-permute-start.24 = (f32[256,1024]{1,0:T(8,128)S(1)}, f32[256,1024]{1,0:T(8,128)S(1)}, u32[]{:S(2)}, u32[]{:S(2)}) collective-permute-start(f32[256,1024]{1,0:T(8,128)S(1)} %dynamic-slice_add_fusion), channel_id=1, source_target_pairs={{0,2},{2,0},{1,3},{3,1},{4,6},{6,4},{5,7},{7,5}} | collective-permute-start | bytes 3145736 | tf_op jit(solution)/shard_map/ppermute | solution.py:679
  1276.5 315.7 %collective-permute-start.32 = (f32[1536,512]{1,0:T(8,128)}, f32[1536,512]{1,0:T(8,128)}, u32[]{:S(2)}, u32[]{:S(2)}) collective-permute-start(f32[1536,512]{1,0:T(8,128)} %get-tuple-element.105.rest_1_), channel_id=1, source_target_pairs={{0,2},{2,0},{1,3},{3,1},{4,6},{6,4},{5,7},{7,5}} | collective-permute-start | bytes 9437192 | tf_op jit(solution)/shard_map/ppermute | solution.py:679
  1367.6 226.0 %collective-permute-start.33 = (f32[1536,512]{1,0:T(8,128)S(1)}, f32[1536,512]{1,0:T(8,128)S(1)}, u32[]{:S(2)}, u32[]{:S(2)}) collective-permute-start(f32[1536,512]{1,0:T(8,128)S(1)} %copy-done.3), channel_id=1, source_target_pairs={{0,1},{1,0},{2,3},{3,2},{4,5},{5,4},{6,7},{7,6}} | collective-permute-start | bytes 9437192 | tf_op jit(solution)/shard_map/ppermute | solution.py:676
  1524.7 73.4 %collective-permute-start.46 = (f32[2096,512]{1,0:T(8,128)}, f32[2096,512]{1,0:T(8,128)}, u32[]{:S(2)}, u32[]{:S(2)}) collective-permute-start(f32[2096,512]{1,0:T(8,128)} %collective-permute-done.45.rest_9_), channel_id=1, source_target_pairs={{0,1},{1,0},{2,3},{3,2},{4,5},{5,4},{6,7},{7,6}} | collective-permute-start | bytes 12877832 | tf_op jit(solution)/shard_map/ppermute | solution.py:676
  1527.0 71.3 %collective-permute-start.49 = (f32[2096,512]{1,0:T(8,128)}, f32[2096,512]{1,0:T(8,128)}, u32[]{:S(2)}, u32[]{:S(2)}) collective-permute-start(f32[2096,512]{1,0:T(8,128)} %collective-permute-done.48.rest_12_), channel_id=1, source_target_pairs={{0,1},{1,0},{2,3},{3,2},{4,5},{5,4},{6,7},{7,6}} | collective-permute-start | bytes 12877832 | tf_op jit(solution)/shard_map/ppermute | solution.py:676
  1527.0 68.3 %collective-permute-start.34 = (f32[1536,512]{1,0:T(8,128)}, f32[1536,512]{1,0:T(8,128)}, u32[]{:S(2)}, u32[]{:S(2)}) collective-permute-start(f32[1536,512]{1,0:T(8,128)} %get-tuple-element.105.rest_1_), channel_id=1, source_target_pairs={{0,1},{1,0},{2,3},{3,2},{4,5},{5,4},{6,7},{7,6}} | collective-permute-start | bytes 9437192 | tf_op jit(solution)/shard_map/ppermute | solution.py:676
  1592.3 3.6 collective-permute-start.25
  1595.3 125.1 %collective-permute-start.52 = (f32[2096,512]{1,0:T(8,128)}, f32[2096,512]{1,0:T(8,128)}, u32[]{:S(2)}, u32[]{:S(2)}) collective-permute-start(f32[2096,512]{1,0:T(8,128)} %collective-permute-done.51), channel_id=1, source_target_pairs={{0,1},{1,0},{2,3},{3,2},{4,5},{5,4},{6,7},{7,6}} | collective-permute-start | bytes 12877832 | tf_op jit(solution)/shard_map/ppermute | solution.py:676
  1595.3 30.3 %collective-permute-start.35 = (f32[1536,512]{1,0:T(8,128)}, f32[1536,512]{1,0:T(8,128)}, u32[]{:S(2)}, u32[]{:S(2)}) collective-permute-start(f32[1536,512]{1,0:T(8,128)} %collective-permute-done.31.rest_2_), channel_id=1, source_target_pairs={{0,1},{1,0},{2,3},{3,2},{4,5},{5,4},{6,7},{7,6}} | collective-permute-start | bytes 9437192 | tf_op jit(solution)/shard_map/ppermute | solution.py:676
  1596.8 28.7 %collective-permute-start.36 = (f32[1536,512]{1,0:T(8,128)}, f32[1536,512]{1,0:T(8,128)}, u32[]{:S(2)}, u32[]{:S(2)}) collective-permute-start(f32[1536,512]{1,0:T(8,128)} %collective-permute-done.32.rest_3_), channel_id=1, source_target_pairs={{0,1},{1,0},{2,3},{3,2},{4,5},{5,4},{6,7},{7,6}} | collective-permute-start | bytes 9437192 | tf_op jit(solution)/shard_map/ppermute | solution.py:676
  1598.2 126.9 %collective-permute-start.29 = (f32[1536,512]{1,0:T(8,128)}, f32[1536,512]{1,0:T(8,128)}, u32[]{:S(2)}, u32[]{:S(2)}) collective-permute-start(f32[1536,512]{1,0:T(8,128)} %get-tuple-element.101.rest_0_), channel_id=1, source_target_pairs={{0,1},{1,0},{2,3},{3,2},{4,5},{5,4},{6,7},{7,6}} | collective-permute-start | bytes 9437192 | tf_op jit(solution)/shard_map/ppermute | solution.py:676
  1598.3 126.8 %collective-permute-start.30 = (f32[1536,512]{1,0:T(8,128)}, f32[1536,512]{1,0:T(8,128)}, u32[]{:S(2)}, u32[]{:S(2)}) collective-permute-start(f32[1536,512]{1,0:T(8,128)} %collective-permute-done.28.rest_1_), channel_id=1, source_target_pairs={{0,1},{1,0},{2,3},{3,2},{4,5},{5,4},{6,7},{7,6}} | collective-permute-start | bytes 9437192 | tf_op jit(solution)/shard_map/ppermute | solution.py:676
  (24 other events, 49.7 us)
